TPU v7x, 32 devices: a whole 2x2x4 slice. The times are simulated.
32 devices in a mesh: sub: 4 (over z), data: 8 (over y, x, core).
Axes of the slice: x: 2, y: 2, z: 4, core: 2. Of those that a mesh axis runs over, the one named last changes fastest.
Arguments:
- x_act: bfloat16 [128, 196, 384], P(('data', 'sub'))
- y_tgt: bfloat16 [128, 196, 384], P(('data', 'sub'))
- w_in: float32 [8, 384, 1536], replicated
- w_out: float32 [8, 1536, 384], replicated
Outputs:
- output 1: float32 [8, 384, 1536], replicated
- output 2: float32 [8, 1536, 384], replicated
- output 3: float32 [], replicated
All inputs are finite; a program needn't handle non-finite values.
Results may differ from a plain program's by a relative error of at most 0.00120099.
Values are sent between devices in bfloat16 or wider.
A program may use at most 1 GiB of HBM per device.

v0:
```python
import jax
import jax.numpy as jnp
from jax import lax
from jax.sharding import PartitionSpec as P

RHO_SCALE = 0.1
STEP_SIZE = 1.0


def gelu_exact(pre_act):
    return jax.nn.gelu(pre_act, approximate=False)


def local_pass(tok_in, tok_tgt, w_in_b, w_out_b):
    layers = w_in_b.shape[0]
    hidden = tok_in
    saved_acts = []
    for layer_idx in range(layers):
        pre_act = jnp.dot(hidden, w_in_b[layer_idx], preferred_element_type=jnp.float32).astype(jnp.bfloat16)
        gelu_out = gelu_exact(pre_act.astype(jnp.float32)).astype(jnp.bfloat16)
        branch = jnp.dot(gelu_out, w_out_b[layer_idx], preferred_element_type=jnp.float32)
        saved_acts.append((hidden, pre_act, gelu_out))
        hidden = (hidden.astype(jnp.float32) + branch).astype(jnp.bfloat16)
    res_diff = hidden.astype(jnp.float32) - tok_tgt.astype(jnp.float32)
    elem_count = res_diff.size
    loss_val = 0.5 * jnp.sum(res_diff * res_diff) / elem_count
    back_err = (res_diff / elem_count).astype(jnp.bfloat16)
    grads_in = []
    grads_out = []
    for layer_idx in reversed(range(layers)):
        hid_in, pre_act, gelu_out = saved_acts[layer_idx]
        grads_out.append(jnp.einsum("tf,td->fd", gelu_out, back_err, preferred_element_type=jnp.float32).astype(jnp.bfloat16))
        d_act = jnp.einsum("td,fd->tf", back_err, w_out_b[layer_idx], preferred_element_type=jnp.float32).astype(jnp.bfloat16)
        gelu_vjp = jax.vjp(gelu_exact, pre_act.astype(jnp.float32))[1]
        d_pre = gelu_vjp(d_act.astype(jnp.float32))[0].astype(jnp.bfloat16)
        grads_in.append(jnp.einsum("td,tf->df", hid_in, d_pre, preferred_element_type=jnp.float32).astype(jnp.bfloat16))
        if layer_idx > 0:
            back_err = (back_err.astype(jnp.float32) + jnp.einsum("tf,df->td", d_pre, w_in_b[layer_idx], preferred_element_type=jnp.float32)).astype(jnp.bfloat16)
    return loss_val, grads_in[::-1], grads_out[::-1]


def solution(mesh):
    sub_size = mesh.shape["sub"]
    dev_count = sub_size * mesh.shape["data"]

    def device_step(x_blk, y_blk, w_in, w_out):
        model_dim = w_in.shape[1]
        tok_in = x_blk.reshape(-1, model_dim)
        tok_tgt = y_blk.reshape(-1, model_dim)
        first_res = local_pass(tok_in, tok_tgt, w_in.astype(jnp.bfloat16), w_out.astype(jnp.bfloat16))
        wide_in = jnp.stack(first_res[1]).astype(jnp.float32)
        wide_out = jnp.stack(first_res[2]).astype(jnp.float32)
        sum_in, sum_out = lax.psum((wide_in, wide_out), "sub")
        mean_in = sum_in / sub_size
        mean_out = sum_out / sub_size
        grad_norm = jnp.sqrt(jnp.sum(mean_in * mean_in) + jnp.sum(mean_out * mean_out))
        eps_scale = RHO_SCALE * model_dim ** 0.5 / grad_norm
        pert_in = (w_in + eps_scale * mean_in).astype(jnp.bfloat16)
        pert_out = (w_out + eps_scale * mean_out).astype(jnp.bfloat16)
        second_res = local_pass(tok_in, tok_tgt, pert_in, pert_out)
        wide2_in = jnp.stack(second_res[1]).astype(jnp.float32)
        wide2_out = jnp.stack(second_res[2]).astype(jnp.float32)
        tot_in, tot_out, tot_loss = lax.psum((wide2_in, wide2_out, second_res[0]), ("sub", "data"))
        return (w_in - STEP_SIZE * (tot_in / dev_count), w_out - STEP_SIZE * (tot_out / dev_count), tot_loss / dev_count)

    batch_spec = P(("data", "sub"))
    return jax.shard_map(device_step, mesh=mesh, in_specs=(batch_spec, batch_spec, P(), P()), out_specs=(P(), P(), P()), check_vma=False)
```

profile of v0, /device:TPU:0, one launch (start us, length us, event | category | flops | bytes accessed | tf_op | source)
XLA Modules:
  0.0 2461.8 jit_solution(597768910843116110)
XLA Ops:
  4.5 7.5 convert_element_type.634
  17.5 11.1 fusion.58
  31.5 12.2 fusion.87
  47.4 12.2 fusion.116
  63.4 12.2 fusion.145
  79.3 12.2 fusion.174
  95.2 12.2 fusion.203
  111.1 12.5 fusion.232
  127.4 13.8 fusion.261
  141.3 5.8 fusion.684
  192.0 7.7 fusion.611
  245.4 18.6 copy.43
  264.1 1244.6 %all-reduce.4 = (f32[8,384,1536]{1,2,0:T(8,128)}, f32[8,1536,384]{2,1,0:T(8,128)}) all-reduce(bf16[8,384,1536]{1,2,0:T(8,128)(2,1)} %fusion.625, bf16[8,1536,384]{2,1,0:T(8,128)(2,1)} %fusion.641), channel_id=1, replica_groups=mesh['sub'=4,'data'=8] {'sub'}, use_global_device_ids=true, to_apply=%region_0.0 | all-reduce | flops 9437184 | bytes 56623104 | tf_op jit(solution)/shard_map/psum | solution.py:53
  1508.7 11.8 multiply_reduce_fusion
  1520.5 11.8 multiply_reduce_fusion.1
  1533.7 12.5 add_convert_fusion
  1546.2 15.9 add_convert_fusion.1
  1562.1 11.3 fusion.350
  1576.4 12.4 fusion.379
  1592.5 12.4 fusion.408
  1608.6 12.4 fusion.437
  1624.7 12.8 fusion.466
  1641.3 12.4 fusion.495
  1657.4 12.4 fusion.524
  1675.0 12.6 fusion.553
  1687.7 5.4 multiply_reduce_fusion.2
  1693.8 8.0 fusion.559
  1741.2 7.7 fusion.643
  1794.4 607.8 %all-reduce.5 = (f32[8,384,1536]{1,2,0:T(8,128)}, f32[8,1536,384]{2,1,0:T(8,128)}, f32[]{:T(128)}) all-reduce(bf16[8,384,1536]{1,2,0:T(8,128)(2,1)} %fusion.657, bf16[8,1536,384]{2,1,0:T(8,128)(2,1)} %fusion.673, f32[]{:T(128)S(6)} %div.47), channel_id=1, replica_groups=mesh['sub'=4,'data'=8] {'sub','data'}, use_global_device_ids=true, to_apply=%region_4.0 | all-reduce | flops 9437185 | bytes 56623112 | tf_op jit(solution)/shard_map/psum | solution.py:63
  2402.8 19.4 multiply_subtract_fusion.1
  2422.2 18.6 copy.44
  2440.8 19.3 multiply_subtract_fusion
  (518 shorter events, 234.2 us)
Async XLA Ops:
  1.9 26.7 %copy-start.7 = (bf16[784,384]{1,0:T(8,128)(2,1)}, bf16[784,384]{1,0:T(8,128)(2,1)S(1)}, u32[]{:S(2)}) copy-start(bf16[784,384]{1,0:T(8,128)(2,1)S(1)} %reshape.12) | copy-start | bytes 1806340
  28.6 15.1 copy-start.18
  43.7 15.9 copy-start.19
  43.8 15.9 copy-start.49
  59.7 15.9 copy-start.20
  59.7 15.9 copy-start.52
  75.6 15.9 copy-start.21
  75.6 15.9 copy-start.55
  91.6 15.9 copy-start.22
  91.6 15.9 copy-start.58
  107.5 55.0 %copy-start.23 = (f32[784,1536]{1,0:T(8,128)}, f32[784,1536]{1,0:T(8,128)S(1)}, u32[]{:S(2)}) copy-start(f32[784,1536]{1,0:T(8,128)S(1)} %get-tuple-element.24) | copy-start | bytes 14450692
  107.5 55.0 %copy-start.61 = (bf16[784,1536]{1,0:T(8,128)(2,1)}, bf16[784,1536]{1,0:T(8,128)(2,1)S(1)}, u32[]{:S(2)}) copy-start(bf16[784,1536]{1,0:T(8,128)(2,1)S(1)} %get-tuple-element.25) | copy-start | bytes 7225348
  123.6 32.0 %copy-start.24 = (f32[784,1536]{1,0:T(8,128)}, f32[784,1536]{1,0:T(8,128)S(1)}, u32[]{:S(2)}) copy-start(f32[784,1536]{1,0:T(8,128)S(1)} %get-tuple-element.26) | copy-start | bytes 14450692
  123.6 32.0 %copy-start.63 = (bf16[784,1536]{1,0:T(8,128)(2,1)}, bf16[784,1536]{1,0:T(8,128)(2,1)S(1)}, u32[]{:S(2)}) copy-start(bf16[784,1536]{1,0:T(8,128)(2,1)S(1)} %get-tuple-element.27) | copy-start | bytes 7225348
  123.6 17.7 slice-start
  127.4 13.9 copy-start.90
  127.4 13.9 slice-start.1
  127.4 13.9 slice-start.2
  1546.2 27.2 %copy-start.2 = (bf16[8,1536,384]{2,1,0:T(8,128)(2,1)}, bf16[8,1536,384]{2,1,0:T(8,128)(2,1)S(1)}, u32[]{:S(2)}) copy-start(bf16[8,1536,384]{2,1,0:T(8,128)(2,1)S(1)} %add_convert_fusion) | copy-start | bytes 28311556
  1573.4 15.4 copy-start.11
  1588.8 16.1 copy-start.12
  1588.8 16.1 copy-start.28
  1604.9 16.1 copy-start.13
  1605.0 16.1 copy-start.31
  1621.1 16.5 copy-start.14
  1621.1 16.5 copy-start.34
  1637.6 16.1 copy-start.15
  1637.6 16.1 copy-start.37
  1653.7 16.1 copy-start.16
  1653.7 59.8 %copy-start.40 = (bf16[784,1536]{1,0:T(8,128)(2,1)}, bf16[784,1536]{1,0:T(8,128)(2,1)S(1)}, u32[]{:S(2)}) copy-start(bf16[784,1536]{1,0:T(8,128)(2,1)S(1)} %get-tuple-element.41) | copy-start | bytes 7225348
  1669.9 17.7 copy-start.42
  1687.6 17.8 slice-start.36
  (174 other events, 915.1 us)
where the time goes:
time: 2470 us; the launch traced here: 2460 us
  blocking collectives  1850 us (75%)
  matrix products  440 us (18%)
  other arithmetic  99.5 us (4%)
  local copies, waits for them, and re-layouts  62.5 us (3%)
    psum x1, blocking collectives, device_step(): sum_in, sum_out = lax.psum((wide_in, wide_out), 'sub')  1240 us
    psum x1, blocking collectives, device_step(): lax.psum((wide2_in, wide2_out, second_res[0]), ('sub', 'data'))  608 us
    dot_general x16, matrix products, local_pass(): jnp.dot(hidden, w_in_b[layer_idx], preferred_element_type=jnp.float32)  197 us
    unnamed x415, local copies, waits for them, and re-layouts  59.9 us
    dot_general x16, matrix products, local_pass(): jnp.einsum('td,tf->df', hid_in, d_pre, preferred_element_type=jnp.float32)  58.9 us
    dot_general x16, matrix products, local_pass(): jnp.dot(gelu_out, w_out_b[layer_idx], preferred_element_type=jnp.float32)  57 us

commit v1 on v0

v1 whole, which is shorter than its diff:
```python
import jax, jax.numpy as jnp, functools
from jax import lax
from jax.experimental import pallas as pl
from jax.experimental.pallas import tpu as pltpu
from jax.sharding import PartitionSpec as P

F32, BF16 = jnp.float32, jnp.bfloat16
RHO_SCALE = 0.1
STEP_SIZE = 1.0
L, T, D, F = 8, 784, 384, 1536
FT = 256
NT = F // FT
RC, CC = 112, 128
SQRT_HALF = 0.5 ** 0.5
INV_SQRT_2PI = 0.3989422804014327


def gelu_only(z):
    return z * (0.5 + 0.5 * lax.erf(z * SQRT_HALF))


def gelu_both(z):
    cdf = 0.5 + 0.5 * lax.erf(z * SQRT_HALF)
    pdf = INV_SQRT_2PI * jnp.exp(-0.5 * (z * z))
    return z * cdf, cdf + z * pdf


def chunks(col0):
    for c in range(FT // CC):
        for r in range(T // RC):
            yield slice(r * RC, (r + 1) * RC), slice(col0 + c * CC, col0 + (c + 1) * CC)


def dot(a, b, ca=1, cb=0):
    return lax.dot_general(a, b, (((ca,), (cb,)), ((), ())), preferred_element_type=F32)


def pass_kernel(x_ref, y_ref, vin_ref, vout_ref, gin_ref, gout_ref, loss_ref, h_s, z_s, a_s, q_s, e_s, hT_s):
    step = pl.program_id(0)

    @pl.when(step == 0)
    def _():
        h_s[0] = x_ref[...]

    @pl.when(step < L)
    def _():
        lay = step
        z_l = z_s.at[lay]
        h = h_s[lay]
        for j in range(NT):
            cols = slice(j * FT, (j + 1) * FT)
            z_l[:, cols] = dot(h, vin_ref[0, :, cols]).astype(BF16)
            for rs, cs in chunks(j * FT):
                a_s[rs, cs] = gelu_only(z_l[rs, cs].astype(F32)).astype(BF16)
        out = (h.astype(F32) + dot(a_s[...], vout_ref[0])).astype(BF16)
        h_s[lay + 1] = out

    @pl.when(step == L - 1)
    def _():
        diff = h_s[L].astype(F32) - y_ref[...].astype(F32)
        loss_ref[0, 0] = 0.5 * jnp.sum(diff * diff) / (T * D)
        e_s[...] = (diff / (T * D)).astype(BF16)

    @pl.when(step >= L)
    def _():
        lay = 2 * L - 1 - step
        z_l = z_s.at[lay]
        e = e_s[...]
        hT_s[...] = h_s[lay].T
        for j in range(NT):
            cols = slice(j * FT, (j + 1) * FT)
            q_s[:, cols] = dot(e, vout_ref[0, cols, :], 1, 1).astype(BF16)
            for rs, cs in chunks(j * FT):
                act, slope = gelu_both(z_l[rs, cs].astype(F32))
                a_s[rs, cs] = act.astype(BF16)
                q_s[rs, cs] = (slope * q_s[rs, cs].astype(F32)).astype(BF16)
            gout_ref[0, cols, :] = dot(a_s[:, cols], e, 0, 0).astype(BF16)
            gin_ref[0, :, cols] = dot(hT_s[...], q_s[:, cols]).astype(BF16)
        e_s[...] = (e.astype(F32) + dot(q_s[...], vin_ref[0], 1, 1)).astype(BF16)


def run_pass(x, y, vin, vout):
    lay = lambda s: jnp.where(s < L, s, 2 * L - 1 - s)
    glay = lambda s: jnp.where(s < L, L - 1, 2 * L - 1 - s)
    return pl.pallas_call(
        pass_kernel,
        grid=(2 * L,),
        in_specs=[
            pl.BlockSpec((T, D), lambda s: (0, 0)),
            pl.BlockSpec((T, D), lambda s: (0, 0)),
            pl.BlockSpec((1, D, F), lambda s: (lay(s), 0, 0)),
            pl.BlockSpec((1, F, D), lambda s: (lay(s), 0, 0)),
        ],
        out_specs=[
            pl.BlockSpec((1, D, F), lambda s: (glay(s), 0, 0)),
            pl.BlockSpec((1, F, D), lambda s: (glay(s), 0, 0)),
            pl.BlockSpec(memory_space=pltpu.SMEM),
        ],
        out_shape=[
            jax.ShapeDtypeStruct((L, D, F), BF16),
            jax.ShapeDtypeStruct((L, F, D), BF16),
            jax.ShapeDtypeStruct((1, 1), F32),
        ],
        scratch_shapes=[
            pltpu.VMEM((L + 1, T, D), BF16),
            pltpu.VMEM((L, T, F), BF16),
            pltpu.VMEM((T, F), BF16),
            pltpu.VMEM((T, F), BF16),
            pltpu.VMEM((T, D), BF16),
            pltpu.VMEM((D, T), BF16),
        ],
        compiler_params=pltpu.CompilerParams(vmem_limit_bytes=60 * 2**20),
        cost_estimate=pl.CostEstimate(flops=L * 12 * T * D * F, bytes_accessed=4 * L * D * F * 2, transcendentals=0),
    )(x, y, vin, vout)


def move_pairs(sub_size, data_size, flip):
    pairs = []
    for shard in range(sub_size):
        for data_idx in range(data_size):
            group = data_idx % 2
            chip = 2 * group + ((shard + flip) % 2)
            pairs.append((shard * data_size + data_idx, chip * data_size + data_idx - group + shard // 2))
    return pairs


def solution(mesh):
    sub_size, data_size = mesh.shape["sub"], mesh.shape["data"]
    dev_count = sub_size * data_size
    axes = ("sub", "data")
    core_swap = [(i, i ^ 1) for i in range(data_size)]

    def swap(v):
        return lax.ppermute(v, "data", core_swap)

    def device_step(x_blk, y_blk, w_in, w_out):
        tok = jnp.stack([x_blk.reshape(T, D), y_blk.reshape(T, D)])
        own = lax.ppermute(tok, axes, move_pairs(sub_size, data_size, 0))
        other = lax.ppermute(tok, axes, move_pairs(sub_size, data_size, 1))
        v_in, v_out = w_in.astype(BF16), w_out.astype(BF16)
        a_in, a_out, _ = run_pass(own[0], own[1], v_in, v_out)
        pa_in, pa_out = swap(a_in), swap(a_out)
        b_in, b_out, _ = run_pass(other[0], other[1], v_in, v_out)
        pb_in, pb_out = swap(b_in), swap(b_out)
        f = lambda v: v.astype(F32)
        mean_in = ((f(a_in) + f(b_in)) + (f(pa_in) + f(pb_in))) / sub_size
        mean_out = ((f(a_out) + f(b_out)) + (f(pa_out) + f(pb_out))) / sub_size
        grad_norm = jnp.sqrt(jnp.sum(mean_in * mean_in) + jnp.sum(mean_out * mean_out))
        scale = RHO_SCALE * D ** 0.5 / grad_norm
        t_in = (w_in + scale * mean_in).astype(BF16)
        t_out = (w_out + scale * mean_out).astype(BF16)
        n_in, n_out, loss = run_pass(own[0], own[1], t_in, t_out)
        idx = lax.axis_index(axes)

        def update(w, g):
            flat = f(g).reshape(-1, g.shape[-1])
            part = lax.psum_scatter(flat, axes, scatter_dimension=0, tiled=True)
            rows = part.shape[0]
            w_part = lax.dynamic_slice_in_dim(w.reshape(flat.shape), idx * rows, rows, 0)
            new = w_part - STEP_SIZE * (part / dev_count)
            return lax.all_gather(new, axes, axis=0, tiled=True).reshape(w.shape)

        return update(w_in, n_in), update(w_out, n_out), lax.psum(loss[0, 0], axes) / dev_count

    batch_spec = P(("data", "sub"))
    return jax.shard_map(device_step, mesh=mesh, in_specs=(batch_spec, batch_spec, P(), P()), out_specs=(P(), P(), P()), check_vma=False)
```

time: 2470 us -> 1150 us (0.47)
  blocking collectives: 1850 us -> 41.1 us
  waiting for transfers between devices: 0 us -> 640 us
  matrix products: 440 us -> 0 us
  Pallas kernels: 0 us -> 269 us
  starting transfers between devices: 0 us -> 32.8 us
  local copies, waits for them, and re-layouts: 62.5 us -> 30.2 us
    psum x2 -> x1, blocking collectives: 1850 us -> 41.1 us  [device_step(): lax.psum(loss[0, 0], axes) / dev_count]
    dot_general x92 -> x0, matrix products: 440 us -> none  [the longest x16 197 us: local_pass(): jnp.dot(hidden, w_in_b[layer_idx], preferred_element_type=jnp.float32)]
    reduce_scatter x0 -> x2, waiting for transfers between devices: none -> 405 us  [update(): part = lax.psum_scatter(flat, axes, scatter_dimension=0, tiled=True)]
    pallas_call x0 -> x3, Pallas kernels: none -> 269 us  [run_pass(): pl.pallas_call(pass_kernel, grid=(2 * L,), in_specs=[pl.BlockSpec((T, D),...]
    all_gather x0 -> x2, waiting for transfers between devices: none -> 210 us  [update(): return lax.all_gather(new, axes, axis=0, tiled=True).reshape(w.shape)]
    sub x2, other arithmetic: 38.7 us -> 4.24 us  [update(): new = w_part - STEP_SIZE * (part / dev_count)]
    ppermute x0 -> x6, starting transfers between devices: none -> 32.6 us  [the longest x4 28.6 us: swap(): return lax.ppermute(v, 'data', core_swap)]
    unnamed x415 -> x23, local copies, waits for them, and re-layouts: 59.9 us -> 27.6 us
  transfers between devices with their start and end apart: 0 -> 10, of which waited for: 0 -> 6; matrix products, arithmetic and copies ran while one was open for 0% -> 4% of each run, Pallas kernels for 0% -> 16%
where the time goes in v1:
time: 1150 us
  waiting for transfers between devices  640 us (56%)
  Pallas kernels  269 us (23%)
  other arithmetic  115 us (10%)
  blocking collectives  41.1 us (4%)
  starting transfers between devices  32.8 us (3%)
  local copies, waits for them, and re-layouts  30.2 us (3%)
  between operations  17.4 us (2%)
    reduce_scatter x2, waiting for transfers between devices, update(): part = lax.psum_scatter(flat, axes, scatter_dimension=0, tiled=True)  405 us
    pallas_call x3, Pallas kernels, run_pass(): pl.pallas_call(pass_kernel, grid=(2 * L,), in_specs=[pl.BlockSpec((T, D),...  269 us
    all_gather x2, waiting for transfers between devices, update(): return lax.all_gather(new, axes, axis=0, tiled=True).reshape(w.shape)  210 us
    psum x1, blocking collectives, device_step(): lax.psum(loss[0, 0], axes) / dev_count  41.1 us
    ppermute x4, starting transfers between devices, swap(): return lax.ppermute(v, 'data', core_swap)  28.6 us
    unnamed x23, local copies, waits for them, and re-layouts  27.6 us
    ppermute x4, waiting for transfers between devices, swap(): return lax.ppermute(v, 'data', core_swap)  25 us
    reshape x2, other arithmetic, update(): flat = f(g).reshape(-1, g.shape[-1])  24.1 us
  transfers between devices with their start and end apart: 10, of which 6 were waited for; matrix products, arithmetic and copies ran while one was open for 4% of the time, Pallas kernels for 16%

profile of v1, /device:TPU:0, one launch (start us, length us, event | category | flops | bytes accessed | tf_op | source)
XLA Modules:
  0.0 1145.4 jit_solution(1122247671102238519)
XLA Ops:
  7.2 1.1 copy.9
  8.6 1.1 copy.10
  9.9 0.9 collective-permute-start
  10.8 3.1 collective-permute-start.1
  14.0 10.6 convert_element_type.38.vin_ref
  24.6 4.4 convert_element_type.39.vout_ref
  28.9 1.2 slice_bitcast_fusion.2
  30.1 86.0 %shard_map.67 = (bf16[8,384,1536]{2,1,0:T(8,128)(2,1)}, bf16[8,1536,384]{2,1,0:T(8,128)(2,1)}, f32[1,1]{1,0:T(1,128)}) custom-call(bf16[784,384]{1,0:T(8,128)(2,1)} %get-tuple-element.20.x_ref, bf16[784,384]{1,0:T(8,128)(2,1)} %get-tuple-element.19.y_ref, bf16[8,384,1536]{2,1,0:T(8,128)(2,1)} %convert_element_type.38.vin_ref, ...), custom_call_target="tpu_custom_call" | custom-call | flops 44392513536 | bytes 37748736 | tf_op jit(solution)/shard_map/pallas_call | solution.py:85
  116.1 27.9 %collective-permute-start.4 = (bf16[8,1536,384]{2,1,0:T(8,128)(2,1)}, bf16[8,1536,384]{2,1,0:T(8,128)(2,1)}, u32[]{:S(2)}, u32[]{:S(2)}) collective-permute-start(bf16[8,1536,384]{2,1,0:T(8,128)(2,1)} %get-tuple-element.12), channel_id=1, source_target_pairs={{0,1},{1,0},{2,3},{3,2},{4,5},{5,4},{6,7},{7,6},{8,9},{9,8},{10,11... | collective-permute-start | bytes 28311560 | tf_op jit(solution)/shard_map/ppermute | solution.py:134
  144.1 1.1 slice_bitcast_fusion
  145.2 96.3 %shard_map.68 = (bf16[8,384,1536]{2,1,0:T(8,128)(2,1)}, bf16[8,1536,384]{2,1,0:T(8,128)(2,1)}, f32[1,1]{1,0:T(1,128)}) custom-call(bf16[784,384]{1,0:T(8,128)(2,1)} %get-tuple-element.18.x_ref, bf16[784,384]{1,0:T(8,128)(2,1)} %get-tuple-element.17.y_ref, bf16[8,384,1536]{2,1,0:T(8,128)(2,1)} %convert_element_type.38.vin_ref, ...), custom_call_target="tpu_custom_call" | custom-call | flops 44392513536 | bytes 37748736 | tf_op jit(solution)/shard_map/pallas_call | solution.py:85
  241.6 0.5 collective-permute-start.2
  242.1 0.1 collective-permute-start.3
  242.3 14.0 %collective-permute-done.5 = bf16[8,1536,384]{2,1,0:T(8,128)(2,1)S(1)} collective-permute-done((bf16[8,1536,384]{2,1,0:T(8,128)(2,1)}, bf16[8,1536,384]{2,1,0:T(8,128)(2,1)S(1)}, u32[]{:S(2)}, u32[]{:S(2)}) %collective-permute-start.5) | collective-permute-done | bytes 9437216 | tf_op jit(solution)/shard_map/ppermute | solution.py:134
  256.2 15.9 %multiply_reduce_fusion = f32[]{:T(128)} fusion(bf16[8,1536,384]{2,1,0:T(8,128)(2,1)S(1)} %collective-permute-done.5, bf16[8,1536,384]{2,1,0:T(8,128)(2,1)} %collective-permute-done.4, bf16[8,1536,384]{2,1,0:T(8,128)(2,1)} %get-tuple-element.13, bf16[8,1536,384]{2,1,0:T(8,128)(2,1)} %get-tuple-element.12), kind=kLoop, calls=%fused_computation.2 | loop fusion | flops 47185920 | bytes 37748740 | tf_op jit(solution)/shard_map/reduce_sum | solution.py:148
  272.2 11.0 collective-permute-done.3
  283.2 11.0 multiply_reduce_fusion.1
  295.5 22.6 %add_convert_fusion.vout_ref = bf16[8,1536,384]{2,1,0:T(8,128)(2,1)} fusion(f32[8,1536,384]{2,1,0:T(8,128)} %param.7, f32[]{:T(128)S(6)} %mul.33, bf16[8,1536,384]{2,1,0:T(8,128)(2,1)} %copy-done.1, bf16[8,1536,384]{2,1,0:T(8,128)(2,1)} %collective-permute-done.4, bf16[8,1536,384]{2,1,0:T(8,128)(2,1)} %get-tuple-element.13, ...), kind=kLoop, calls=%fused_computation | loop fusion | flops 47185920 | bytes 66060292 | tf_op jit(solution)/shard_map/convert_element_type | solution.py:151
  318.1 22.5 %add_convert_fusion.1.vin_ref = bf16[8,384,1536]{2,1,0:T(8,128)(2,1)} fusion(f32[8,384,1536]{2,1,0:T(8,128)} %param.6, f32[]{:T(128)S(6)} %mul.33, bf16[8,384,1536]{2,1,0:T(8,128)(2,1)} %collective-permute-done.3, bf16[8,384,1536]{2,1,0:T(8,128)(2,1)} %collective-permute-done.2, bf16[8,384,1536]{2,1,0:T(8,128)(2,1)} %get-tuple-element.11, ...), kind=kLoop, calls=%fused_computation.1 | loop fusion | flops 47185920 | bytes 66060292 | tf_op jit(solution)/shard_map/convert_element_type | solution.py:150
  340.6 86.2 %shard_map.69 = (bf16[8,384,1536]{2,1,0:T(8,128)(2,1)}, bf16[8,1536,384]{2,1,0:T(8,128)(2,1)}, f32[1,1]{1,0:T(1,128)}) custom-call(bf16[784,384]{1,0:T(8,128)(2,1)} %get-tuple-element.20.x_ref, bf16[784,384]{1,0:T(8,128)(2,1)} %get-tuple-element.19.y_ref, bf16[8,384,1536]{2,1,0:T(8,128)(2,1)} %add_convert_fusion.1.vin_ref, ...), custom_call_target="tpu_custom_call" | custom-call | flops 44392513536 | bytes 37748736 | tf_op jit(solution)/shard_map/pallas_call | solution.py:85
  426.9 10.8 bitcast_convert_fusion
  437.8 13.2 %bitcast_convert_fusion.1 = f32[3072,1536]{1,0:T(8,128)} fusion(bf16[8,384,1536]{2,1,0:T(8,128)(2,1)} %get-tuple-element.14), kind=kLoop, calls=%fused_computation.7 | loop fusion | flops 4718592 | bytes 28311552 | tf_op jit(solution)/shard_map/reshape | solution.py:156
  451.1 194.7 %reduce-scatter.5.cloned.1.call-done = f32[384,384]{1,0:T(8,128)} async-done(((f32[12288,384]{1,0:T(8,128)}), f32[384,384]{1,0:T(8,128)}) %reduce-scatter.5.cloned.1.call-update) | async-done | bytes 589840 | tf_op jit(solution)/shard_map/reduce_scatter | solution.py:157
  645.8 2.1 multiply_subtract_fusion
  648.0 210.7 %reduce-scatter.3.cloned.1.call-done = f32[96,1536]{1,0:T(8,128)} async-done(((f32[3072,1536]{1,0:T(8,128)}), f32[96,1536]{1,0:T(8,128)}) %reduce-scatter.3.cloned.1.call-update) | async-done | bytes 589840 | tf_op jit(solution)/shard_map/reduce_scatter | solution.py:157
  858.7 2.1 multiply_subtract_fusion.1
  860.8 41.1 %psum.7 = f32[]{:T(128)} all-reduce(f32[]{:T(128)} %bitcast.10), channel_id=1, replica_groups=mesh['sub'=4,'data'=8] {'sub','data'}, use_global_device_ids=true, to_apply=%region_4.0 | all-reduce | flops 1 | bytes 8 | tf_op jit(solution)/shard_map/psum | solution.py:163
  902.6 84.1 %all-gather.5.cloned.1.call-done = f32[12288,384]{1,0:T(8,128)} async-done(((f32[384,384]{1,0:T(8,128)}), f32[12288,384]{1,0:T(8,128)}) %all-gather.5.cloned.1.call-update) | async-done | bytes 18874384 | tf_op jit(solution)/shard_map/all_gather | solution.py:161
  986.7 125.4 %all-gather.3.cloned.1.call-done = f32[3072,1536]{1,0:T(8,128)} async-done(((f32[96,1536]{1,0:T(8,128)}), f32[3072,1536]{1,0:T(8,128)}) %all-gather.3.cloned.1.call-update) | async-done | bytes 18874384 | tf_op jit(solution)/shard_map/all_gather | solution.py:161
  1112.1 13.7 %copy.14 = f32[8,384,1536]{2,1,0:T(8,128)} copy(f32[8,384,1536]{2,1,0:T(8,128)} %bitcast.26) | data formatting | bytes 37748736
  1125.9 4.6 copy-done.2
  1130.5 6.8 copy.15
  (36 shorter events, 0.7 us)
Async XLA Ops:
  7.2 638.6 %reduce-scatter.5.cloned.1.call-start = ((), (), s32[]{:S(2)}) async-start(), calls=%async_computation.4 | async-start | bytes 19464192 | tf_op jit(solution)/shard_map/reduce_scatter | solution.py:157
  9.8 14.7 %copy-start = (f32[8,1536,384]{2,1,0:T(8,128)S(1)}, f32[8,1536,384]{2,1,0:T(8,128)}, u32[]{:S(2)}) copy-start(f32[8,1536,384]{2,1,0:T(8,128)} %param.7) | copy-start | bytes 56623108
  9.9 19.0 %collective-permute-start = (bf16[2,784,384]{2,1,0:T(8,128)(2,1)S(1)}, bf16[2,784,384]{2,1,0:T(8,128)(2,1)S(1)}, u32[]{:S(2)}, u32[]{:S(2)}) collective-permute-start(bf16[2,784,384]{2,1,0:T(8,128)(2,1)S(1)} %constant_dynamic-update-slice_fusion), channel_id=1, source_target_pairs={{0,0},{1,16},{2,2},{3,18},{4,4},{5,20},{6,6},{7,22},{8,8},{9,24},{... | collective-permute-start | bytes 3612680 | tf_op jit(solution)/shard_map/ppermute | solution.py:138
  10.8 133.3 %collective-permute-start.1 = (bf16[2,784,384]{2,1,0:T(8,128)(2,1)S(1)}, bf16[2,784,384]{2,1,0:T(8,128)(2,1)S(1)}, u32[]{:S(2)}, u32[]{:S(2)}) collective-permute-start(bf16[2,784,384]{2,1,0:T(8,128)(2,1)S(1)} %constant_dynamic-update-slice_fusion), channel_id=1, source_target_pairs={{0,8},{1,24},{2,10},{3,26},{4,12},{5,28},{6,14},{7,30},{8,0},{9,16... | collective-permute-start | bytes 3612680 | tf_op jit(solution)/shard_map/ppermute | solution.py:139
  116.1 126.1 %collective-permute-start.4 = (bf16[8,1536,384]{2,1,0:T(8,128)(2,1)}, bf16[8,1536,384]{2,1,0:T(8,128)(2,1)}, u32[]{:S(2)}, u32[]{:S(2)}) collective-permute-start(bf16[8,1536,384]{2,1,0:T(8,128)(2,1)} %get-tuple-element.12), channel_id=1, source_target_pairs={{0,1},{1,0},{2,3},{3,2},{4,5},{5,4},{6,7},{7,6},{8,9},{9,8},{10,11... | collective-permute-start | bytes 28311560 | tf_op jit(solution)/shard_map/ppermute | solution.py:134
  241.6 14.7 %collective-permute-start.5 = (bf16[8,1536,384]{2,1,0:T(8,128)(2,1)}, bf16[8,1536,384]{2,1,0:T(8,128)(2,1)S(1)}, u32[]{:S(2)}, u32[]{:S(2)}) collective-permute-start(bf16[8,1536,384]{2,1,0:T(8,128)(2,1)} %get-tuple-element.13), channel_id=1, source_target_pairs={{0,1},{1,0},{2,3},{3,2},{4,5},{5,4},{6,7},{7,6},{8,9},{9,8},{10,11... | collective-permute-start | bytes 28311560 | tf_op jit(solution)/shard_map/ppermute | solution.py:134
  241.6 30.6 %collective-permute-start.2 = (bf16[8,384,1536]{2,1,0:T(8,128)(2,1)}, bf16[8,384,1536]{2,1,0:T(8,128)(2,1)}, u32[]{:S(2)}, u32[]{:S(2)}) collective-permute-start(bf16[8,384,1536]{2,1,0:T(8,128)(2,1)} %get-tuple-element.10), channel_id=1, source_target_pairs={{0,1},{1,0},{2,3},{3,2},{4,5},{5,4},{6,7},{7,6},{8,9},{9,8},{10,11... | collective-permute-start | bytes 28311560 | tf_op jit(solution)/shard_map/ppermute | solution.py:134
  242.1 41.1 %slice-start = ((s8[9437184]{0:T(1024)(128)(4,1)}), s8[4194304]{0:T(1024)(128)(4,1)S(1)}, s32[]{:S(2)}) async-start(s8[9437184]{0:T(1024)(128)(4,1)} %bitcast.21), calls=%async_computation.6 | async-start | bytes 8388608
  242.1 41.1 %slice-start.3 = ((s8[9437184]{0:T(1024)(128)(4,1)}), s8[4194304]{0:T(1024)(128)(4,1)S(1)}, s32[]{:S(2)}) async-start(s8[9437184]{0:T(1024)(128)(4,1)} %bitcast.23), calls=%async_computation.9 | async-start | bytes 8388608
  242.1 41.1 %slice-start.1 = ((s8[9437184]{0:T(1024)(128)(4,1)}), s8[4194304]{0:T(1024)(128)(4,1)S(1)}, s32[]{:S(2)}) async-start(s8[9437184]{0:T(1024)(128)(4,1)} %bitcast.21), calls=%async_computation.7 | async-start | bytes 8388608
  242.1 41.1 %slice-start.2 = ((s8[9437184]{0:T(1024)(128)(4,1)}), s8[1048576]{0:T(1024)(128)(4,1)S(1)}, s32[]{:S(2)}) async-start(s8[9437184]{0:T(1024)(128)(4,1)} %bitcast.21), calls=%async_computation.8 | async-start | bytes 2097152
  242.1 41.1 %slice-start.4 = ((s8[9437184]{0:T(1024)(128)(4,1)}), s8[4194304]{0:T(1024)(128)(4,1)S(1)}, s32[]{:S(2)}) async-start(s8[9437184]{0:T(1024)(128)(4,1)} %bitcast.23), calls=%async_computation.10 | async-start | bytes 8388608
  242.1 41.1 %slice-start.5 = ((s8[9437184]{0:T(1024)(128)(4,1)}), s8[1048576]{0:T(1024)(128)(4,1)S(1)}, s32[]{:S(2)}) async-start(s8[9437184]{0:T(1024)(128)(4,1)} %bitcast.23), calls=%async_computation.11 | async-start | bytes 2097152
  242.1 41.1 %collective-permute-start.3 = (bf16[8,384,1536]{2,1,0:T(8,128)(2,1)}, bf16[8,384,1536]{2,1,0:T(8,128)(2,1)}, u32[]{:S(2)}, u32[]{:S(2)}) collective-permute-start(bf16[8,384,1536]{2,1,0:T(8,128)(2,1)} %get-tuple-element.11), channel_id=1, source_target_pairs={{0,1},{1,0},{2,3},{3,2},{4,5},{5,4},{6,7},{7,6},{8,9},{9,8},{10,11... | collective-permute-start | bytes 28311560 | tf_op jit(solution)/shard_map/ppermute | solution.py:134
  256.2 15.9 %copy-start.1 = (bf16[8,1536,384]{2,1,0:T(8,128)(2,1)}, bf16[8,1536,384]{2,1,0:T(8,128)(2,1)S(1)}, u32[]{:S(2)}) copy-start(bf16[8,1536,384]{2,1,0:T(8,128)(2,1)S(1)} %collective-permute-done.5) | copy-start | bytes 28311556
  437.7 420.9 %reduce-scatter.3.cloned.1.call-start = ((), (), s32[]{:S(2)}) async-start(), calls=%async_computation.2 | async-start | bytes 19464192 | tf_op jit(solution)/shard_map/reduce_scatter | solution.py:157
  451.0 535.7 %all-gather.5.cloned.1.call-start = ((), (), s32[]{:S(2)}) async-start(), calls=%async_computation.5 | async-start | bytes 19464192 | tf_op jit(solution)/shard_map/all_gather | solution.py:161
  647.9 464.2 %all-gather.3.cloned.1.call-start = ((), (), s32[]{:S(2)}) async-start(), calls=%async_computation.3 | async-start | bytes 19464192 | tf_op jit(solution)/shard_map/all_gather | solution.py:161
  1112.1 18.4 %copy-start.2 = (f32[12288,384]{1,0:T(8,128)S(1)}, f32[12288,384]{1,0:T(8,128)}, u32[]{:S(2)}) copy-start(f32[12288,384]{1,0:T(8,128)} %all-gather.5.cloned.1.call-done) | copy-start | bytes 56623108
Sparse Core Ops, SparseCore 0:
  437.8 207.8 reduce-scatter.4
  652.8 205.8 reduce-scatter.2
  862.1 124.5 all-gather.4
  990.0 122.0 all-gather.2

commit v2 on v1

--- a/solution.py
+++ b/solution.py
@@ -114,6 +114,424 @@
     )(x, y, vin, vout)
 
 
+ROWS = (384, 768)
+COLS = (768, 384)
+STAGES = 7
+MESH_ID = pl.DeviceIdType.MESH
+
+
+def al(v, n):
+    return pl.multiple_of(v, n)
+
+
+def half_at(ref, kind, lay, core, row, rows):
+    if kind == 0:
+        return ref.at[lay, pl.ds(al(row, 8), rows), pl.ds(al(core * COLS[0], 128), COLS[0])]
+    return ref.at[lay, pl.ds(al(core * ROWS[1] + row, 8), rows), :]
+
+
+def row_loop(rows, block, body):
+    def step(i, _):
+        body(al(i * block, block))
+        return 0
+    lax.fori_loop(0, rows // block, step, 0)
+
+
+class Place:
+    def __init__(self):
+        z, data = lax.axis_index("sub"), lax.axis_index("data")
+        core, xx, yy = lax.rem(data, 2), lax.rem(data // 2, 2), data // 4
+        self.core, self.z = core, z
+        flips = (2 - 4 * xx, 4 - 8 * yy)
+        self.partner = (z, data + 1 - 2 * core)
+        self.first = tuple((z, data + f) for f in flips)
+        self.second = (self.first[1], self.first[0])
+        self.c1, self.c2 = (xx, yy), (yy, xx)
+        self.zs = [lax.rem(z + d, 4) for d in (1, 2, 3)]
+        self.z_peers = [(zt, data) for zt in self.zs]
+
+    def barrier(self, peers):
+        sem = pltpu.get_barrier_semaphore()
+        for peer in peers:
+            pl.semaphore_signal(sem, inc=1, device_id=peer, device_id_type=MESH_ID)
+        pl.semaphore_wait(sem, len(peers))
+
+
+def remote(src, dst, send, recv, peer):
+    return pltpu.make_async_remote_copy(src_ref=src, dst_ref=dst, send_sem=send, recv_sem=recv, device_id=peer, device_id_type=MESH_ID)
+
+
+def exch_kernel(count, g0, g1, w0, w1, loss_ref, o0, o1, lout,
+                own0, own1, d0, d1, r10, r11, r20, r21, r30, r31, s10, s11, s20, s21, s30, s31, nb0, nb1, wb0, wb1, lt, lr,
+                own_sem, w_sem, d_sem, r1_sem, r2_sem, r3_sem, az_sem, a2_sem, a1_sem, ad_sem,
+                ds_sem, s1_sem, s2_sem, s3_sem, zs_sem, n_sem, a2s_sem, a1s_sem, ads_sem, l_sem, ls_sem):
+    me = Place()
+    core, z = me.core, me.z
+    g, w, o = (g0, g1), (w0, w1), (o0, o1)
+    own, dd, r1, r2, r3 = (own0, own1), (d0, d1), (r10, r11), (r20, r21), (r30, r31)
+    s1, s2, s3, nb, wb = (s10, s11), (s20, s21), (s30, s31), (nb0, nb1), (wb0, wb1)
+    kinds = (0, 1)
+    me.barrier([me.partner, me.first[0], me.first[1]] + me.z_peers)
+
+    def quarter(kind):
+        return (2 * me.c1[kind] + me.c2[kind]) * (ROWS[kind] // 4)
+
+    def own_copy(l, k):
+        return pltpu.make_async_copy(half_at(g[k], k, l, core, 0, ROWS[k]), own[k].at[l], own_sem.at[l, k])
+
+    def w_copy(l, k):
+        n = ROWS[k] // 16
+        return pltpu.make_async_copy(half_at(w[k], k, l, core, quarter(k) + z * n, n), wb[k].at[l], w_sem.at[l, k])
+
+    def d_copy(l, k):
+        return remote(half_at(g[k], k, l, 1 - core, 0, ROWS[k]), dd[k].at[l], ds_sem.at[l, k], d_sem.at[l, k], me.partner)
+
+    def r1_copy(l, k):
+        slot = lax.rem(l, 2)
+        return remote(s1[k].at[slot], r1[k].at[l], s1_sem.at[slot, k], r1_sem.at[l, k], me.first[k])
+
+    def r2_copy(l, k):
+        slot = lax.rem(l, 2)
+        return remote(s2[k].at[slot], r2[k].at[l], s2_sem.at[slot, k], r2_sem.at[l, k], me.second[k])
+
+    def r3_copy(l, k, j):
+        slot, n = lax.rem(l, 2), ROWS[k] // 16
+        return remote(s3[k].at[slot, pl.ds(al(me.zs[j] * n, 8), n)], r3[k].at[l, 2 - j], s3_sem.at[slot, k, j], r3_sem.at[l, k, 2 - j], me.z_peers[j])
+
+    def piece(l, k, zi):
+        n = ROWS[k] // 16
+        return half_at(o[k], k, l, core, quarter(k) + zi * n, n)
+
+    def az_copy(l, k, j):
+        slot = lax.rem(l, 2)
+        return remote(nb[k].at[slot], piece(l, k, z), zs_sem.at[slot, k, j], az_sem.at[l, k, 2 - j], me.z_peers[j])
+
+    def n_copy(l, k):
+        slot = lax.rem(l, 2)
+        return pltpu.make_async_copy(nb[k].at[slot], piece(l, k, z), n_sem.at[slot, k])
+
+    def gather(l, k, row, rows, send, recv, peer):
+        part = half_at(o[k], k, l, core, row, rows)
+        return remote(part, part, send.at[lax.rem(l, 2), k], recv.at[l, k], peer)
+
+    def a2_copy(l, k):
+        return gather(l, k, quarter(k), ROWS[k] // 4, a2s_sem, a2_sem, me.second[k])
+
+    def a1_copy(l, k):
+        return gather(l, k, me.c1[k] * (ROWS[k] // 2), ROWS[k] // 2, a1s_sem, a1_sem, me.first[k])
+
+    def ad_copy(l, k):
+        return gather(l, k, 0, ROWS[k], ads_sem, ad_sem, me.partner)
+
+    def both(k, l, row, n):
+        return own[k][l, pl.ds(row, n), :].astype(F32) + dd[k][l, pl.ds(row, n), :].astype(F32)
+
+    def start(l, k):
+        d_copy(l, k).start()
+        own_copy(l, k).start()
+        w_copy(l, k).start()
+
+    def stage0(l, k):
+        own_copy(l, k).wait()
+        d_copy(l, k).wait_recv()
+
+        @pl.when(l >= 2)
+        def _():
+            r1_copy(l - 2, k).wait_send()
+        n, slot = ROWS[k] // 2, lax.rem(l, 2)
+        base = (1 - me.c1[k]) * n
+
+        def body(row):
+            s1[k][slot, pl.ds(row, 16), :] = both(k, l, al(base + row, 16), 16)
+        row_loop(n, 16, body)
+        r1_copy(l, k).start()
+
+    def stage1(l, k):
+        r1_copy(l, k).wait_recv()
+
+        @pl.when(l >= 2)
+        def _():
+            r2_copy(l - 2, k).wait_send()
+        n, slot = ROWS[k] // 4, lax.rem(l, 2)
+        in_half = (1 - me.c2[k]) * n
+        base = me.c1[k] * 2 * n + in_half
+
+        def body(row):
+            s2[k][slot, pl.ds(row, 16), :] = both(k, l, al(base + row, 16), 16) + r1[k][l, pl.ds(al(in_half + row, 16), 16), :]
+        row_loop(n, 16, body)
+        r2_copy(l, k).start()
+
+    def stage2(l, k):
+        r2_copy(l, k).wait_recv()
+
+        @pl.when(l >= 2)
+        def _():
+            for j in range(3):
+                r3_copy(l - 2, k, j).wait_send()
+        n, slot = ROWS[k] // 4, lax.rem(l, 2)
+        in_half = me.c2[k] * n
+        base = me.c1[k] * 2 * n + in_half
+
+        def body(row):
+            s3[k][slot, pl.ds(row, 16), :] = (both(k, l, al(base + row, 16), 16) + r1[k][l, pl.ds(al(in_half + row, 16), 16), :]) + r2[k][l, pl.ds(row, 16), :]
+        row_loop(n, 16, body)
+        for j in range(3):
+            r3_copy(l, k, j).start()
+
+    def stage3(l, k):
+        for j in range(3):
+            r3_copy(l, k, j).wait_recv()
+        w_copy(l, k).wait()
+
+        @pl.when(l >= 2)
+        def _():
+            for j in range(3):
+                az_copy(l - 2, k, j).wait_send()
+        n, slot = ROWS[k] // 16, lax.rem(l, 2)
+
+        def body(row):
+            rs = pl.ds(row, 8)
+            tot = (s3[k][slot, pl.ds(al(z * n + row, 8), 8), :] + r3[k][l, 0, rs, :]) + (r3[k][l, 1, rs, :] + r3[k][l, 2, rs, :])
+            nb[k][slot, rs, :] = wb[k][l, rs, :] - STEP_SIZE * (tot * (1.0 / count))
+        row_loop(n, 8, body)
+        n_copy(l, k).start()
+        for j in range(3):
+            az_copy(l, k, j).start()
+
+    def stage4(l, k):
+        n_copy(l, k).wait()
+        for j in range(3):
+            az_copy(l, k, j).wait_recv()
+
+        @pl.when(l >= 2)
+        def _():
+            a2_copy(l - 2, k).wait_send()
+        a2_copy(l, k).start()
+
+    def stage5(l, k):
+        a2_copy(l, k).wait_recv()
+
+        @pl.when(l >= 2)
+        def _():
+            a1_copy(l - 2, k).wait_send()
+        a1_copy(l, k).start()
+
+    def stage6(l, k):
+        a1_copy(l, k).wait_recv()
+
+        @pl.when(l >= 2)
+        def _():
+            ad_copy(l - 2, k).wait_send()
+        ad_copy(l, k).start()
+
+    stages = (stage0, stage1, stage2, stage3, stage4, stage5, stage6)
+
+    def loss_copy(i, peer, j):
+        return remote(lt.at[i], lr.at[j], ls_sem.at[j], l_sem.at[j], peer)
+
+    loss_hops = [[(me.partner, 0)], [(me.first[0], 1)], [(me.first[1], 2)], [(me.z_peers[j], 3 + j) for j in range(3)]]
+
+    def loss_wait(i):
+        for peer, j in loss_hops[i]:
+            loss_copy(i, peer, j).wait()
+        tot = lt[i]
+        for _, j in loss_hops[i]:
+            tot = tot + (lr[j] if i < 3 else lr[8 - j])
+        return tot
+
+    lt[0] = jnp.full((8, 128), loss_ref[0, 0], F32)
+
+    def start_all(l, _):
+        for k in kinds:
+            start(l, k)
+        return 0
+    lax.fori_loop(0, L, start_all, 0)
+
+    def loss_step(t):
+        for i in range(5):
+            @pl.when(t == i)
+            def _(i=i):
+                if i > 0:
+                    tot = loss_wait(i - 1)
+                    if i == 4:
+                        lout[...] = tot * (1.0 / count)
+                    else:
+                        lt[i] = tot
+                if i < 4:
+                    for peer, j in loss_hops[i]:
+                        loss_copy(i, peer, j).start()
+
+    def tick(t, _):
+        loss_step(t)
+        for s in reversed(range(STAGES)):
+            l = t - s
+
+            @pl.when(jnp.logical_and(l >= 0, l < L))
+            def _(s=s, l=l):
+                for k in kinds:
+                    stages[s](l, k)
+        return 0
+    lax.fori_loop(0, L + STAGES - 1, tick, 0)
+
+    def finish(l, _):
+        for k in kinds:
+            ad_copy(l, k).wait_recv()
+            d_copy(l, k).wait_send()
+        return 0
+    lax.fori_loop(0, L, finish, 0)
+    for l in (L - 2, L - 1):
+        for k in kinds:
+            r1_copy(l, k).wait_send()
+            r2_copy(l, k).wait_send()
+            for j in range(3):
+                r3_copy(l, k, j).wait_send()
+                az_copy(l, k, j).wait_send()
+            a2_copy(l, k).wait_send()
+            a1_copy(l, k).wait_send()
+            ad_copy(l, k).wait_send()
+
+
+def exchange(count, g_in, g_out, w_in, w_out, loss):
+    def per_kind(lead, div, dtype):
+        return [pltpu.VMEM(lead + (ROWS[k] // div, COLS[k]), dtype) for k in (0, 1)]
+    dma = pltpu.SemaphoreType.DMA
+    any_spec = pl.BlockSpec(memory_space=pl.ANY)
+    scratch = (per_kind((L,), 1, BF16) + per_kind((L,), 1, BF16) + per_kind((L,), 2, F32) + per_kind((L,), 4, F32)
+               + per_kind((L, 3), 16, F32) + per_kind((2,), 2, F32) + per_kind((2,), 4, F32) + per_kind((2,), 4, F32)
+               + per_kind((2,), 16, F32) + per_kind((L,), 16, F32) + [pltpu.VMEM((4, 8, 128), F32), pltpu.VMEM((6, 8, 128), F32)]
+               + [dma((L, 2))] * 5 + [dma((L, 2, 3))] * 2 + [dma((L, 2))] * 4
+               + [dma((2, 2))] * 2 + [dma((2, 2, 3))] * 2 + [dma((2, 2))] * 4 + [dma((6,))] * 2)
+    return pl.pallas_call(
+        functools.partial(exch_kernel, count),
+        in_specs=[any_spec] * 4 + [pl.BlockSpec(memory_space=pltpu.SMEM)],
+        out_specs=[any_spec, any_spec, pl.BlockSpec(memory_space=pltpu.VMEM)],
+        out_shape=[jax.ShapeDtypeStruct((L, D, F), F32), jax.ShapeDtypeStruct((L, F, D), F32), jax.ShapeDtypeStruct((8, 128), F32)],
+        scratch_shapes=scratch,
+        compiler_params=pltpu.CompilerParams(collective_id=1, has_side_effects=True, vmem_limit_bytes=60 * 2**20),
+    )(g_in, g_out, w_in, w_out, loss)
+
+
+def ascent_kernel(group, a0, a1, b0, b1, w0, w1, t0, t1, oa0, oa1, ob0, ob1, pa0, pa1, pb0, pb1, wb0, wb1, tb0, tb1, nt,
+                  o_sem, p_sem, ps_sem, w_sem, tl_sem, ts_sem, tr_sem, n_sem):
+    me = Place()
+    core = me.core
+    src, w, t = ((a0, a1), (b0, b1)), (w0, w1), (t0, t1)
+    own, peer = ((oa0, oa1), (ob0, ob1)), ((pa0, pa1), (pb0, pb1))
+    wb, tb, kinds = (wb0, wb1), (tb0, tb1), (0, 1)
+    me.barrier([me.partner])
+
+    def own_copy(l, k, i):
+        return pltpu.make_async_copy(half_at(src[i][k], k, l, core, 0, ROWS[k]), own[i][k].at[l], o_sem.at[l, k, i])
+
+    def peer_copy(l, k, i):
+        return remote(half_at(src[i][k], k, l, 1 - core, 0, ROWS[k]), peer[i][k].at[l], ps_sem.at[l, k, i], p_sem.at[l, k, i], me.partner)
+
+    def w_copy(l, k):
+        slot = lax.rem(l, 2)
+        return pltpu.make_async_copy(half_at(w[k], k, l, core, 0, ROWS[k]), wb[k].at[slot], w_sem.at[slot, k])
+
+    def t_half(l, k):
+        return half_at(t[k], k, l, core, 0, ROWS[k])
+
+    def t_local(l, k):
+        slot = lax.rem(l, 2)
+        return pltpu.make_async_copy(tb[k].at[slot], t_half(l, k), tl_sem.at[slot, k])
+
+    def t_send(l, k):
+        slot = lax.rem(l, 2)
+        return remote(tb[k].at[slot], t_half(l, k), ts_sem.at[slot, k], tr_sem.at[l, k], me.partner)
+
+    def mean_rows(l, k, row):
+        rs = pl.ds(row, 16)
+        f = lambda ref: ref[l, rs, :].astype(F32)
+        return ((f(own[0][k]) + f(own[1][k])) + (f(peer[0][k]) + f(peer[1][k]))) * (1.0 / group)
+
+    def start_all(l, _):
+        for k in kinds:
+            for i in range(2):
+                peer_copy(l, k, i).start()
+                own_copy(l, k, i).start()
+        return 0
+    lax.fori_loop(0, L, start_all, 0)
+    for l in range(2):
+        for k in kinds:
+            w_copy(l, k).start()
+
+    def square_layer(l, acc):
+        for k in kinds:
+            for i in range(2):
+                own_copy(l, k, i).wait()
+                peer_copy(l, k, i).wait_recv()
+
+            def body(i, tot, k=k):
+                g = mean_rows(l, k, al(i * 16, 16))
+                sq = g * g
+                parts = [sq[r:r + 8, c:c + 128] for r in (0, 8) for c in range(0, COLS[k], 128)]
+                while len(parts) > 1:
+                    parts = [u + v for u, v in zip(parts[::2], parts[1::2])] + parts[len(parts) & ~1:]
+                return tot + parts[0]
+            acc = lax.fori_loop(0, ROWS[k] // 16, body, acc)
+        return acc
+    nt[0] = lax.fori_loop(0, L, square_layer, jnp.zeros((8, 128), F32))
+    norm_copy = remote(nt.at[0], nt.at[1], n_sem.at[0], n_sem.at[1], me.partner)
+    norm_copy.start()
+    norm_copy.wait()
+    total = jnp.sum(jnp.sum(nt[0] + nt[1], axis=0, keepdims=True), axis=1, keepdims=True)
+    scale = (RHO_SCALE * D ** 0.5) / jnp.sqrt(total)
+
+    def move_layer(l, _):
+        for k in kinds:
+            slot = lax.rem(l, 2)
+            w_copy(l, k).wait()
+
+            @pl.when(l >= 2)
+            def _(k=k):
+                t_local(l - 2, k).wait()
+                t_send(l - 2, k).wait_send()
+
+            def body(row, k=k, slot=slot):
+                rs = pl.ds(row, 16)
+                tb[k][slot, rs, :] = (wb[k][slot, rs, :] + scale * mean_rows(l, k, row)).astype(BF16)
+            row_loop(ROWS[k], 16, body)
+            t_send(l, k).start()
+            t_local(l, k).start()
+
+            @pl.when(l < L - 2)
+            def _(k=k):
+                w_copy(l + 2, k).start()
+        return 0
+    lax.fori_loop(0, L, move_layer, 0)
+
+    def finish(l, _):
+        for k in kinds:
+            t_send(l, k).wait_recv()
+            for i in range(2):
+                peer_copy(l, k, i).wait_send()
+        return 0
+    lax.fori_loop(0, L, finish, 0)
+    for l in (L - 2, L - 1):
+        for k in kinds:
+            t_local(l, k).wait()
+            t_send(l, k).wait_send()
+
+
+def ascent(group, first, second, w_in, w_out):
+    def per_kind(lead, dtype):
+        return [pltpu.VMEM((lead, ROWS[k], COLS[k]), dtype) for k in (0, 1)]
+    dma = pltpu.SemaphoreType.DMA
+    any_spec = pl.BlockSpec(memory_space=pl.ANY)
+    scratch = (per_kind(L, BF16) * 4 + per_kind(2, F32) + per_kind(2, BF16) + [pltpu.VMEM((2, 8, 128), F32)]
+               + [dma((L, 2, 2))] * 3 + [dma((2, 2))] * 3 + [dma((L, 2)), dma((2,))])
+    return pl.pallas_call(
+        functools.partial(ascent_kernel, group),
+        in_specs=[any_spec] * 6,
+        out_specs=[any_spec] * 2,
+        out_shape=[jax.ShapeDtypeStruct((L, D, F), BF16), jax.ShapeDtypeStruct((L, F, D), BF16)],
+        scratch_shapes=scratch,
+        compiler_params=pltpu.CompilerParams(collective_id=2, has_side_effects=True, vmem_limit_bytes=60 * 2**20),
+    )(*first, *second, w_in, w_out)
+
+
 def move_pairs(sub_size, data_size, flip):
     pairs = []
     for shard in range(sub_size):
@@ -128,39 +546,18 @@
     sub_size, data_size = mesh.shape["sub"], mesh.shape["data"]
     dev_count = sub_size * data_size
     axes = ("sub", "data")
-    core_swap = [(i, i ^ 1) for i in range(data_size)]
-
-    def swap(v):
-        return lax.ppermute(v, "data", core_swap)
 
     def device_step(x_blk, y_blk, w_in, w_out):
         tok = jnp.stack([x_blk.reshape(T, D), y_blk.reshape(T, D)])
         own = lax.ppermute(tok, axes, move_pairs(sub_size, data_size, 0))
         other = lax.ppermute(tok, axes, move_pairs(sub_size, data_size, 1))
         v_in, v_out = w_in.astype(BF16), w_out.astype(BF16)
-        a_in, a_out, _ = run_pass(own[0], own[1], v_in, v_out)
-        pa_in, pa_out = swap(a_in), swap(a_out)
-        b_in, b_out, _ = run_pass(other[0], other[1], v_in, v_out)
-        pb_in, pb_out = swap(b_in), swap(b_out)
-        f = lambda v: v.astype(F32)
-        mean_in = ((f(a_in) + f(b_in)) + (f(pa_in) + f(pb_in))) / sub_size
-        mean_out = ((f(a_out) + f(b_out)) + (f(pa_out) + f(pb_out))) / sub_size
-        grad_norm = jnp.sqrt(jnp.sum(mean_in * mean_in) + jnp.sum(mean_out * mean_out))
-        scale = RHO_SCALE * D ** 0.5 / grad_norm
-        t_in = (w_in + scale * mean_in).astype(BF16)
-        t_out = (w_out + scale * mean_out).astype(BF16)
+        first = run_pass(own[0], own[1], v_in, v_out)[:2]
+        second = run_pass(other[0], other[1], v_in, v_out)[:2]
+        t_in, t_out = ascent(sub_size, first, second, w_in, w_out)
         n_in, n_out, loss = run_pass(own[0], own[1], t_in, t_out)
-        idx = lax.axis_index(axes)
-
-        def update(w, g):
-            flat = f(g).reshape(-1, g.shape[-1])
-            part = lax.psum_scatter(flat, axes, scatter_dimension=0, tiled=True)
-            rows = part.shape[0]
-            w_part = lax.dynamic_slice_in_dim(w.reshape(flat.shape), idx * rows, rows, 0)
-            new = w_part - STEP_SIZE * (part / dev_count)
-            return lax.all_gather(new, axes, axis=0, tiled=True).reshape(w.shape)
-
-        return update(w_in, n_in), update(w_out, n_out), lax.psum(loss[0, 0], axes) / dev_count
+        new_in, new_out, loss_all = exchange(dev_count, n_in, n_out, w_in, w_out, loss)
+        return new_in, new_out, loss_all[0, 0]
 
     batch_spec = P(("data", "sub"))
     return jax.shard_map(device_step, mesh=mesh, in_specs=(batch_spec, batch_spec, P(), P()), out_specs=(P(), P(), P()), check_vma=False)

time: 1150 us -> 693 us (0.60)
  waiting for transfers between devices: 640 us -> 9.59 us
  Pallas kernels: 269 us -> 632 us
  other arithmetic: 115 us -> 15 us
  blocking collectives: 41.1 us -> 0 us
  starting transfers between devices: 32.8 us -> 4.01 us
  between operations: 17.4 us -> 0.71 us
    reduce_scatter x2 -> x0, waiting for transfers between devices: 405 us -> none  [update(): part = lax.psum_scatter(flat, axes, scatter_dimension=0, tiled=True)]
    pallas_call x0 -> x2, Pallas kernels: none -> 374 us  [the longest x1 325 us: exchange(): pl.pallas_call(functools.partial(exch_kernel, count), in_specs=[any_spec]...]
    all_gather x2 -> x0, waiting for transfers between devices: 210 us -> none  [update(): return lax.all_gather(new, axes, axis=0, tiled=True).reshape(w.shape)]
    convert_element_type x2 -> x0, other arithmetic: 45.1 us -> none  [the longest x1 22.6 us: device_step(): t_out = (w_out + scale * mean_out).astype(BF16)]
    psum x1 -> x0, blocking collectives: 41.1 us -> none  [device_step(): lax.psum(loss[0, 0], axes) / dev_count]
    ppermute x4 -> x0, starting transfers between devices: 28.6 us -> none  [swap(): return lax.ppermute(v, 'data', core_swap)]
    reduce_sum x2 -> x0, other arithmetic: 26.9 us -> none  [the longest x1 15.9 us: device_step(): jnp.sum(mean_out * mean_out)]
    ppermute x4 -> x0, waiting for transfers between devices: 25 us -> none  [swap(): return lax.ppermute(v, 'data', core_swap)]
  transfers between devices with their start and end apart: 10 -> 2, of which waited for: 6 -> 1; matrix products, arithmetic and copies ran while one was open for 4% -> 2% of each run, Pallas kernels for 16% -> 12%
where the time goes in v2:
time: 693 us
  Pallas kernels  632 us (91%)
  local copies, waits for them, and re-layouts  31.4 us (5%)
  other arithmetic  15 us (2%)
  waiting for transfers between devices  9.59 us (1%)
    pallas_call x1, Pallas kernels, exchange(): pl.pallas_call(functools.partial(exch_kernel, count), in_specs=[any_spec]...  325 us
    pallas_call x3, Pallas kernels, run_pass(): pl.pallas_call(pass_kernel, grid=(2 * L,), in_specs=[pl.BlockSpec((T, D),...  258 us
    pallas_call x1, Pallas kernels, ascent(): pl.pallas_call(functools.partial(ascent_kernel, group), in_specs=[any_spe...  48.9 us
    unnamed x9, local copies, waits for them, and re-layouts  27.6 us
    convert_element_type x2, other arithmetic, device_step(): v_in, v_out = (w_in.astype(BF16), w_out.astype(BF16))  15 us
  transfers between devices with their start and end apart: 2, of which 1 were waited for; matrix products, arithmetic and copies ran while one was open for 2% of the time, Pallas kernels for 12%

profile of v2, /device:TPU:0, one launch (start us, length us, event | category | flops | bytes accessed | tf_op | source)
XLA Modules:
  0.0 692.7 jit_solution(11339245652676255707)
XLA Ops:
  0.6 1.1 copy.9
  1.8 0.1 stack_reshape.6
  1.9 0.1 constant_dynamic-update-slice_fusion.1
  2.0 1.1 copy.10
  3.1 0.1 stack_reshape.7
  3.2 0.1 constant_dynamic-update-slice_fusion
  3.3 0.0 copy-start
  3.4 3.1 collective-permute-start.1
  6.5 0.9 collective-permute-start
  7.4 10.6 %convert_element_type.6.vin_ref = bf16[8,384,1536]{2,1,0:T(8,128)(2,1)} convert(f32[8,384,1536]{2,1,0:T(8,128)} %w0.3) | non-fusion elementwise | flops 4718592 | bytes 28311552 | tf_op jit(solution)/shard_map/convert_element_type | solution.py:554
  18.0 0.0 copy-done
  18.0 4.4 convert_element_type.7.vout_ref
  22.3 9.6 %collective-permute-done.1 = bf16[2,784,384]{2,1,0:T(8,128)(2,1)S(1)} collective-permute-done((bf16[2,784,384]{2,1,0:T(8,128)(2,1)S(1)}, bf16[2,784,384]{2,1,0:T(8,128)(2,1)S(1)}, u32[]{:S(2)}, u32[]{:S(2)}) %collective-permute-start.1) | collective-permute-done | bytes 1204256 | tf_op jit(solution)/shard_map/ppermute | solution.py:553
  31.9 1.1 slice_bitcast_fusion
  33.1 86.0 %shard_map.68 = (bf16[8,384,1536]{2,1,0:T(8,128)(2,1)}, bf16[8,1536,384]{2,1,0:T(8,128)(2,1)}, f32[1,1]{1,0:T(1,128)}) custom-call(bf16[784,384]{1,0:T(8,128)(2,1)} %get-tuple-element.28.x_ref, bf16[784,384]{1,0:T(8,128)(2,1)} %get-tuple-element.27.y_ref, bf16[8,384,1536]{2,1,0:T(8,128)(2,1)} %convert_element_type.6.vin_ref, ...), custom_call_target="tpu_custom_call" | custom-call | flops 44392513536 | bytes 37748736 | tf_op jit(solution)/shard_map/pallas_call | solution.py:85
  119.1 0.0 collective-permute-done
  119.1 1.2 slice_bitcast_fusion.2
  120.3 86.0 %shard_map.67 = (bf16[8,384,1536]{2,1,0:T(8,128)(2,1)}, bf16[8,1536,384]{2,1,0:T(8,128)(2,1)}, f32[1,1]{1,0:T(1,128)}) custom-call(bf16[784,384]{1,0:T(8,128)(2,1)} %get-tuple-element.30.x_ref, bf16[784,384]{1,0:T(8,128)(2,1)} %get-tuple-element.29.y_ref, bf16[8,384,1536]{2,1,0:T(8,128)(2,1)} %convert_element_type.6.vin_ref, ...), custom_call_target="tpu_custom_call" | custom-call | flops 44392513536 | bytes 37748736 | tf_op jit(solution)/shard_map/pallas_call | solution.py:85
  206.3 48.9 %shard_map.69 = (bf16[8,384,1536]{2,1,0:T(8,128)(2,1)}, bf16[8,1536,384]{2,1,0:T(8,128)(2,1)}) custom-call(bf16[8,384,1536]{2,1,0:T(8,128)(2,1)} %get-tuple-element.15.a0, bf16[8,1536,384]{2,1,0:T(8,128)(2,1)} %get-tuple-element.16.a1, bf16[8,384,1536]{2,1,0:T(8,128)(2,1)} %get-tuple-element.17.b0, bf16[8,1536,384]{2,1,0:T(8,128)(2,1)} %get-tuple-element.18.b1, ...), custom_call_target="tpu_custom_call" | custom-call | tf_op jit(solution)/shard_map/pallas_call | solution.py:525
  255.2 86.2 %shard_map.70 = (bf16[8,384,1536]{2,1,0:T(8,128)(2,1)}, bf16[8,1536,384]{2,1,0:T(8,128)(2,1)}, f32[1,1]{1,0:T(1,128)}) custom-call(bf16[784,384]{1,0:T(8,128)(2,1)} %get-tuple-element.30.x_ref, bf16[784,384]{1,0:T(8,128)(2,1)} %get-tuple-element.29.y_ref, bf16[8,384,1536]{2,1,0:T(8,128)(2,1)} %get-tuple-element.19.vin_ref, ...), custom_call_target="tpu_custom_call" | custom-call | flops 44392513536 | bytes 37748736 | tf_op jit(solution)/shard_map/pallas_call | solution.py:85
  341.4 324.9 %shard_map.71 = (f32[8,384,1536]{2,1,0:T(8,128)}, f32[8,1536,384]{2,1,0:T(8,128)}, f32[8,128]{1,0:T(8,128)}) custom-call(bf16[8,384,1536]{2,1,0:T(8,128)(2,1)} %get-tuple-element.21.g0, bf16[8,1536,384]{2,1,0:T(8,128)(2,1)} %get-tuple-element.22.g1, f32[8,384,1536]{2,1,0:T(8,128)} %w0.3, f32[8,1536,384]{2,1,0:T(8,128)} %w1.3, f32[1,1]{1,0:T(1,128)} %get-tuple-element.23.loss_ref), custom_call_target="tpu_custom_call" | custom-call | tf_op jit(solution)/shard_map/pallas_call | solution.py:404
  666.3 1.2 slice.21
  667.5 0.0 copy-start.1
  667.5 13.7 %copy.14 = f32[8,384,1536]{2,1,0:T(8,128)} copy(f32[8,384,1536]{2,1,0:T(8,128)} %get-tuple-element.34) | data formatting | bytes 37748736
  681.2 4.6 copy-done.1
  685.8 6.8 copy.15
Async XLA Ops:
  3.3 14.6 %copy-start = (f32[8,1536,384]{2,1,0:T(8,128)S(1)}, f32[8,1536,384]{2,1,0:T(8,128)}, u32[]{:S(2)}) copy-start(f32[8,1536,384]{2,1,0:T(8,128)} %w1.3) | copy-start | bytes 56623108
  3.4 28.6 %collective-permute-start.1 = (bf16[2,784,384]{2,1,0:T(8,128)(2,1)S(1)}, bf16[2,784,384]{2,1,0:T(8,128)(2,1)S(1)}, u32[]{:S(2)}, u32[]{:S(2)}) collective-permute-start(bf16[2,784,384]{2,1,0:T(8,128)(2,1)S(1)} %constant_dynamic-update-slice_fusion), channel_id=1, source_target_pairs={{0,8},{1,24},{2,10},{3,26},{4,12},{5,28},{6,14},{7,30},{8,0},{9,16... | collective-permute-start | bytes 3612680 | tf_op jit(solution)/shard_map/ppermute | solution.py:553
  6.5 112.6 %collective-permute-start = (bf16[2,784,384]{2,1,0:T(8,128)(2,1)S(1)}, bf16[2,784,384]{2,1,0:T(8,128)(2,1)S(1)}, u32[]{:S(2)}, u32[]{:S(2)}) collective-permute-start(bf16[2,784,384]{2,1,0:T(8,128)(2,1)S(1)} %constant_dynamic-update-slice_fusion), channel_id=1, source_target_pairs={{0,0},{1,16},{2,2},{3,18},{4,4},{5,20},{6,6},{7,22},{8,8},{9,24},{... | collective-permute-start | bytes 3612680 | tf_op jit(solution)/shard_map/ppermute | solution.py:552
  667.5 18.4 %copy-start.1 = (f32[8,1536,384]{2,1,0:T(8,128)S(1)}, f32[8,1536,384]{2,1,0:T(8,128)}, u32[]{:S(2)}) copy-start(f32[8,1536,384]{2,1,0:T(8,128)} %get-tuple-element.35) | copy-start | bytes 56623108

commit v3 on v2

--- a/solution.py
+++ b/solution.py
@@ -161,30 +161,28 @@
     return pltpu.make_async_remote_copy(src_ref=src, dst_ref=dst, send_sem=send, recv_sem=recv, device_id=peer, device_id_type=MESH_ID)
 
 
-def exch_kernel(count, g0, g1, w0, w1, loss_ref, o0, o1, lout,
-                own0, own1, d0, d1, r10, r11, r20, r21, r30, r31, s10, s11, s20, s21, s30, s31, nb0, nb1, wb0, wb1, lt, lr,
-                own_sem, w_sem, d_sem, r1_sem, r2_sem, r3_sem, az_sem, a2_sem, a1_sem, ad_sem,
+def last_kernel(count, x_ref, y_ref, vin_ref, vout_ref, w0, w1, o0, o1, lout, h_s, z_s, a_s, q_s, e_s, hT_s, gs0, gs1,
+                d0, d1, r10, r11, r20, r21, r30, r31, s10, s11, s20, s21, s30, s31, nb0, nb1, wb0, wb1, lt, lr,
+                w_sem, d_sem, r1_sem, r2_sem, r3_sem, az_sem, a2_sem, a1_sem, ad_sem,
                 ds_sem, s1_sem, s2_sem, s3_sem, zs_sem, n_sem, a2s_sem, a1s_sem, ads_sem, l_sem, ls_sem):
+    step = pl.program_id(0)
     me = Place()
     core, z = me.core, me.z
-    g, w, o = (g0, g1), (w0, w1), (o0, o1)
-    own, dd, r1, r2, r3 = (own0, own1), (d0, d1), (r10, r11), (r20, r21), (r30, r31)
+    gs, w, o = (gs0, gs1), (w0, w1), (o0, o1)
+    dd, r1, r2, r3 = (d0, d1), (r10, r11), (r20, r21), (r30, r31)
     s1, s2, s3, nb, wb = (s10, s11), (s20, s21), (s30, s31), (nb0, nb1), (wb0, wb1)
     kinds = (0, 1)
-    me.barrier([me.partner, me.first[0], me.first[1]] + me.z_peers)
 
     def quarter(kind):
         return (2 * me.c1[kind] + me.c2[kind]) * (ROWS[kind] // 4)
 
-    def own_copy(l, k):
-        return pltpu.make_async_copy(half_at(g[k], k, l, core, 0, ROWS[k]), own[k].at[l], own_sem.at[l, k])
-
     def w_copy(l, k):
         n = ROWS[k] // 16
-        return pltpu.make_async_copy(half_at(w[k], k, l, core, quarter(k) + z * n, n), wb[k].at[l], w_sem.at[l, k])
+        return pltpu.make_async_copy(half_at(w[k], k, L - 1 - l, core, quarter(k) + z * n, n), wb[k].at[l], w_sem.at[l, k])
 
     def d_copy(l, k):
-        return remote(half_at(g[k], k, l, 1 - core, 0, ROWS[k]), dd[k].at[l], ds_sem.at[l, k], d_sem.at[l, k], me.partner)
+        slot = lax.rem(l, 3)
+        return remote(half_at(gs[k], k, slot, 1 - core, 0, ROWS[k]), dd[k].at[l], ds_sem.at[slot, k], d_sem.at[l, k], me.partner)
 
     def r1_copy(l, k):
         slot = lax.rem(l, 2)
@@ -200,7 +198,7 @@
 
     def piece(l, k, zi):
         n = ROWS[k] // 16
-        return half_at(o[k], k, l, core, quarter(k) + zi * n, n)
+        return half_at(o[k], k, L - 1 - l, core, quarter(k) + zi * n, n)
 
     def az_copy(l, k, j):
         slot = lax.rem(l, 2)
@@ -211,7 +209,7 @@
         return pltpu.make_async_copy(nb[k].at[slot], piece(l, k, z), n_sem.at[slot, k])
 
     def gather(l, k, row, rows, send, recv, peer):
-        part = half_at(o[k], k, l, core, row, rows)
+        part = half_at(o[k], k, L - 1 - l, core, row, rows)
         return remote(part, part, send.at[lax.rem(l, 2), k], recv.at[l, k], peer)
 
     def a2_copy(l, k):
@@ -224,15 +222,14 @@
         return gather(l, k, 0, ROWS[k], ads_sem, ad_sem, me.partner)
 
     def both(k, l, row, n):
-        return own[k][l, pl.ds(row, n), :].astype(F32) + dd[k][l, pl.ds(row, n), :].astype(F32)
-
-    def start(l, k):
-        d_copy(l, k).start()
-        own_copy(l, k).start()
-        w_copy(l, k).start()
+        slot = lax.rem(l, 3)
+        if k == 0:
+            mine = gs[0][slot, pl.ds(row, n), pl.ds(al(core * COLS[0], 128), COLS[0])]
+        else:
+            mine = gs[1][slot, pl.ds(al(core * ROWS[1] + row, 16), n), :]
+        return mine.astype(F32) + dd[k][l, pl.ds(row, n), :].astype(F32)
 
     def stage0(l, k):
-        own_copy(l, k).wait()
         d_copy(l, k).wait_recv()
 
         @pl.when(l >= 2)
@@ -339,13 +336,10 @@
             tot = tot + (lr[j] if i < 3 else lr[8 - j])
         return tot
 
-    lt[0] = jnp.full((8, 128), loss_ref[0, 0], F32)
-
     def start_all(l, _):
         for k in kinds:
-            start(l, k)
+            w_copy(l, k).start()
         return 0
-    lax.fori_loop(0, L, start_all, 0)
 
     def loss_step(t):
         for i in range(5):
@@ -363,6 +357,11 @@
 
     def tick(t, _):
         loss_step(t)
+
+        @pl.when(t < L)
+        def _():
+            for k in kinds:
+                d_copy(t, k).start()
         for s in reversed(range(STAGES)):
             l = t - s
 
@@ -371,44 +370,105 @@
                 for k in kinds:
                     stages[s](l, k)
         return 0
-    lax.fori_loop(0, L + STAGES - 1, tick, 0)
-
-    def finish(l, _):
-        for k in kinds:
-            ad_copy(l, k).wait_recv()
-            d_copy(l, k).wait_send()
-        return 0
-    lax.fori_loop(0, L, finish, 0)
-    for l in (L - 2, L - 1):
-        for k in kinds:
-            r1_copy(l, k).wait_send()
-            r2_copy(l, k).wait_send()
-            for j in range(3):
-                r3_copy(l, k, j).wait_send()
-                az_copy(l, k, j).wait_send()
-            a2_copy(l, k).wait_send()
-            a1_copy(l, k).wait_send()
-            ad_copy(l, k).wait_send()
-
-
-def exchange(count, g_in, g_out, w_in, w_out, loss):
+
+    @pl.when(step == 0)
+    def _():
+        me.barrier([me.partner, me.first[0], me.first[1]] + me.z_peers)
+        h_s[0] = x_ref[...]
+        lax.fori_loop(0, L, start_all, 0)
+
+    @pl.when(step < L)
+    def _():
+        h = h_s[step]
+        for j in range(NT):
+            cols = slice(j * FT, (j + 1) * FT)
+            z_s[:, cols] = dot(h, vin_ref[0, :, cols]).astype(BF16)
+            for rs, cs in chunks(j * FT):
+                a_s[rs, cs] = gelu_only(z_s[rs, cs].astype(F32)).astype(BF16)
+        h_s[step + 1] = (h.astype(F32) + dot(a_s[...], vout_ref[0])).astype(BF16)
+
+    @pl.when(step == L - 1)
+    def _():
+        diff = h_s[L].astype(F32) - y_ref[...].astype(F32)
+        lt[0] = jnp.full((8, 128), 0.5 * jnp.sum(diff * diff) / (T * D), F32)
+        e_s[...] = (diff / (T * D)).astype(BF16)
+
+    @pl.when(step >= L)
+    def _():
+        item = step - L
+        slot = lax.rem(item, 3)
+        lay = L - 1 - item
+
+        @pl.when(item >= 3)
+        def _():
+            for k in kinds:
+                d_copy(item - 3, k).wait_send()
+        e, h = e_s[...], h_s[lay]
+        hT_s[...] = h.T
+        for j in range(NT):
+            cols = slice(j * FT, (j + 1) * FT)
+            z_s[:, cols] = dot(h, vin_ref[0, :, cols]).astype(BF16)
+            q_s[:, cols] = dot(e, vout_ref[0, cols, :], 1, 1).astype(BF16)
+            for rs, cs in chunks(j * FT):
+                act, slope = gelu_both(z_s[rs, cs].astype(F32))
+                a_s[rs, cs] = act.astype(BF16)
+                q_s[rs, cs] = (slope * q_s[rs, cs].astype(F32)).astype(BF16)
+            gs1[slot, cols, :] = dot(a_s[:, cols], e, 0, 0).astype(BF16)
+            gs0[slot, :, cols] = dot(hT_s[...], q_s[:, cols]).astype(BF16)
+        e_s[...] = (e.astype(F32) + dot(q_s[...], vin_ref[0], 1, 1)).astype(BF16)
+        lax.fori_loop(item, jnp.where(item == L - 1, L + STAGES - 1, item + 1), tick, 0)
+
+    @pl.when(step == 2 * L - 1)
+    def _():
+        def finish(l, _):
+            for k in kinds:
+                ad_copy(l, k).wait_recv()
+            return 0
+        lax.fori_loop(0, L, finish, 0)
+        for l in (L - 3, L - 2, L - 1):
+            for k in kinds:
+                d_copy(l, k).wait_send()
+        for l in (L - 2, L - 1):
+            for k in kinds:
+                r1_copy(l, k).wait_send()
+                r2_copy(l, k).wait_send()
+                for j in range(3):
+                    r3_copy(l, k, j).wait_send()
+                    az_copy(l, k, j).wait_send()
+                a2_copy(l, k).wait_send()
+                a1_copy(l, k).wait_send()
+                ad_copy(l, k).wait_send()
+
+
+def last_pass(count, x, y, vin, vout, w_in, w_out):
     def per_kind(lead, div, dtype):
         return [pltpu.VMEM(lead + (ROWS[k] // div, COLS[k]), dtype) for k in (0, 1)]
     dma = pltpu.SemaphoreType.DMA
     any_spec = pl.BlockSpec(memory_space=pl.ANY)
-    scratch = (per_kind((L,), 1, BF16) + per_kind((L,), 1, BF16) + per_kind((L,), 2, F32) + per_kind((L,), 4, F32)
+    lay = lambda s: jnp.where(s < L, s, 2 * L - 1 - s)
+    scratch = ([pltpu.VMEM((L + 1, T, D), BF16)] + [pltpu.VMEM((T, F), BF16)] * 3 + [pltpu.VMEM((T, D), BF16), pltpu.VMEM((D, T), BF16)]
+               + [pltpu.VMEM((3, D, F), BF16), pltpu.VMEM((3, F, D), BF16)]
+               + per_kind((L,), 1, BF16) + per_kind((L,), 2, F32) + per_kind((L,), 4, F32)
                + per_kind((L, 3), 16, F32) + per_kind((2,), 2, F32) + per_kind((2,), 4, F32) + per_kind((2,), 4, F32)
                + per_kind((2,), 16, F32) + per_kind((L,), 16, F32) + [pltpu.VMEM((4, 8, 128), F32), pltpu.VMEM((6, 8, 128), F32)]
-               + [dma((L, 2))] * 5 + [dma((L, 2, 3))] * 2 + [dma((L, 2))] * 4
+               + [dma((L, 2))] * 4 + [dma((L, 2, 3))] * 2 + [dma((L, 2))] * 3 + [dma((3, 2))]
                + [dma((2, 2))] * 2 + [dma((2, 2, 3))] * 2 + [dma((2, 2))] * 4 + [dma((6,))] * 2)
     return pl.pallas_call(
-        functools.partial(exch_kernel, count),
-        in_specs=[any_spec] * 4 + [pl.BlockSpec(memory_space=pltpu.SMEM)],
-        out_specs=[any_spec, any_spec, pl.BlockSpec(memory_space=pltpu.VMEM)],
+        functools.partial(last_kernel, count),
+        grid=(2 * L,),
+        in_specs=[
+            pl.BlockSpec((T, D), lambda s: (0, 0), pipeline_mode=pl.Buffered(1)),
+            pl.BlockSpec((T, D), lambda s: (0, 0), pipeline_mode=pl.Buffered(1)),
+            pl.BlockSpec((1, D, F), lambda s: (lay(s), 0, 0)),
+            pl.BlockSpec((1, F, D), lambda s: (lay(s), 0, 0)),
+            any_spec,
+            any_spec,
+        ],
+        out_specs=[any_spec, any_spec, pl.BlockSpec((8, 128), lambda s: (0, 0))],
         out_shape=[jax.ShapeDtypeStruct((L, D, F), F32), jax.ShapeDtypeStruct((L, F, D), F32), jax.ShapeDtypeStruct((8, 128), F32)],
         scratch_shapes=scratch,
-        compiler_params=pltpu.CompilerParams(collective_id=1, has_side_effects=True, vmem_limit_bytes=60 * 2**20),
-    )(g_in, g_out, w_in, w_out, loss)
+        compiler_params=pltpu.CompilerParams(collective_id=1, has_side_effects=True, vmem_limit_bytes=67_000_000),
+    )(x, y, vin, vout, w_in, w_out)
 
 
 def ascent_kernel(group, a0, a1, b0, b1, w0, w1, t0, t1, oa0, oa1, ob0, ob1, pa0, pa1, pb0, pb1, wb0, wb1, tb0, tb1, nt,
@@ -555,8 +615,7 @@
         first = run_pass(own[0], own[1], v_in, v_out)[:2]
         second = run_pass(other[0], other[1], v_in, v_out)[:2]
         t_in, t_out = ascent(sub_size, first, second, w_in, w_out)
-        n_in, n_out, loss = run_pass(own[0], own[1], t_in, t_out)
-        new_in, new_out, loss_all = exchange(dev_count, n_in, n_out, w_in, w_out, loss)
+        new_in, new_out, loss_all = last_pass(dev_count, own[0], own[1], t_in, t_out, w_in, w_out)
         return new_in, new_out, loss_all[0, 0]
 
     batch_spec = P(("data", "sub"))

time: 693 us -> 640 us (0.924)
  Pallas kernels: 632 us -> 580 us
    pallas_call x3 -> x2, Pallas kernels: 258 us -> 172 us  [run_pass(): pl.pallas_call(pass_kernel, grid=(2 * L,), in_specs=[pl.BlockSpec((T, D),...]
    pallas_call x1, Pallas kernels: 325 us -> 359 us  [last_pass(): pl.pallas_call(functools.partial(last_kernel, count), grid=(2 * L,), in_s...]
  transfers between devices with their start and end apart: 2 -> 2, of which waited for: 1 -> 1; matrix products, arithmetic and copies ran while one was open for 2% -> 3% of each run, Pallas kernels for 12% -> 13%
where the time goes in v3:
time: 640 us
  Pallas kernels  580 us (91%)
  local copies, waits for them, and re-layouts  31.4 us (5%)
  other arithmetic  15 us (2%)
  waiting for transfers between devices  9.59 us (1%)
    pallas_call x1, Pallas kernels, last_pass(): pl.pallas_call(functools.partial(last_kernel, count), grid=(2 * L,), in_s...  359 us
    pallas_call x2, Pallas kernels, run_pass(): pl.pallas_call(pass_kernel, grid=(2 * L,), in_specs=[pl.BlockSpec((T, D),...  172 us
    pallas_call x1, Pallas kernels, ascent(): pl.pallas_call(functools.partial(ascent_kernel, group), in_specs=[any_spe...  48.9 us
    unnamed x9, local copies, waits for them, and re-layouts  27.6 us
    convert_element_type x2, other arithmetic, device_step(): v_in, v_out = (w_in.astype(BF16), w_out.astype(BF16))  15 us
  transfers between devices with their start and end apart: 2, of which 1 were waited for; matrix products, arithmetic and copies ran while one was open for 3% of the time, Pallas kernels for 13%

profile of v3, /device:TPU:0, one launch (start us, length us, event | category | flops | bytes accessed | tf_op | source)
XLA Modules:
  0.0 640.3 jit_solution(16429990781501722873)
XLA Ops:
  0.6 1.1 copy.9
  1.8 0.1 stack_reshape.6
  1.9 0.1 constant_dynamic-update-slice_fusion.1
  2.0 1.1 copy.10
  3.1 0.1 stack_reshape.7
  3.2 0.1 constant_dynamic-update-slice_fusion
  3.3 0.0 copy-start
  3.4 3.1 collective-permute-start.1
  6.5 0.9 collective-permute-start
  7.4 10.6 %convert_element_type.6.vin_ref = bf16[8,384,1536]{2,1,0:T(8,128)(2,1)} convert(f32[8,384,1536]{2,1,0:T(8,128)} %w0.3) | non-fusion elementwise | flops 4718592 | bytes 28311552 | tf_op jit(solution)/shard_map/convert_element_type | solution.py:614
  18.0 0.0 copy-done
  18.0 4.4 convert_element_type.7.vout_ref
  22.3 9.6 %collective-permute-done.1 = bf16[2,784,384]{2,1,0:T(8,128)(2,1)S(1)} collective-permute-done((bf16[2,784,384]{2,1,0:T(8,128)(2,1)S(1)}, bf16[2,784,384]{2,1,0:T(8,128)(2,1)S(1)}, u32[]{:S(2)}, u32[]{:S(2)}) %collective-permute-start.1) | collective-permute-done | bytes 1204256 | tf_op jit(solution)/shard_map/ppermute | solution.py:613
  31.9 1.1 slice_bitcast_fusion
  33.1 86.0 %shard_map.68 = (bf16[8,384,1536]{2,1,0:T(8,128)(2,1)}, bf16[8,1536,384]{2,1,0:T(8,128)(2,1)}, f32[1,1]{1,0:T(1,128)}) custom-call(bf16[784,384]{1,0:T(8,128)(2,1)} %get-tuple-element.22.x_ref, bf16[784,384]{1,0:T(8,128)(2,1)} %get-tuple-element.21.y_ref, bf16[8,384,1536]{2,1,0:T(8,128)(2,1)} %convert_element_type.6.vin_ref, ...), custom_call_target="tpu_custom_call" | custom-call | flops 44392513536 | bytes 37748736 | tf_op jit(solution)/shard_map/pallas_call | solution.py:85
  119.1 0.0 collective-permute-done
  119.1 1.2 slice_bitcast_fusion.2
  120.3 86.0 %shard_map.67 = (bf16[8,384,1536]{2,1,0:T(8,128)(2,1)}, bf16[8,1536,384]{2,1,0:T(8,128)(2,1)}, f32[1,1]{1,0:T(1,128)}) custom-call(bf16[784,384]{1,0:T(8,128)(2,1)} %get-tuple-element.24.x_ref, bf16[784,384]{1,0:T(8,128)(2,1)} %get-tuple-element.23.y_ref, bf16[8,384,1536]{2,1,0:T(8,128)(2,1)} %convert_element_type.6.vin_ref, ...), custom_call_target="tpu_custom_call" | custom-call | flops 44392513536 | bytes 37748736 | tf_op jit(solution)/shard_map/pallas_call | solution.py:85
  206.2 48.9 %shard_map.69 = (bf16[8,384,1536]{2,1,0:T(8,128)(2,1)}, bf16[8,1536,384]{2,1,0:T(8,128)(2,1)}) custom-call(bf16[8,384,1536]{2,1,0:T(8,128)(2,1)} %get-tuple-element.12.a0, bf16[8,1536,384]{2,1,0:T(8,128)(2,1)} %get-tuple-element.13.a1, bf16[8,384,1536]{2,1,0:T(8,128)(2,1)} %get-tuple-element.14.b0, bf16[8,1536,384]{2,1,0:T(8,128)(2,1)} %get-tuple-element.15.b1, ...), custom_call_target="tpu_custom_call" | custom-call | tf_op jit(solution)/shard_map/pallas_call | solution.py:585
  255.1 358.7 %shard_map.70 = (f32[8,384,1536]{2,1,0:T(8,128)}, f32[8,1536,384]{2,1,0:T(8,128)}, f32[8,128]{1,0:T(8,128)}) custom-call(bf16[784,384]{1,0:T(8,128)(2,1)} %get-tuple-element.24.x_ref, bf16[784,384]{1,0:T(8,128)(2,1)} %get-tuple-element.23.y_ref, bf16[8,384,1536]{2,1,0:T(8,128)(2,1)} %get-tuple-element.16.vin_ref, ...), custom_call_target="tpu_custom_call" | custom-call | tf_op jit(solution)/shard_map/pallas_call | solution.py:456
  613.9 1.2 slice.21
  615.0 0.0 copy-start.1
  615.0 13.7 %copy.14 = f32[8,384,1536]{2,1,0:T(8,128)} copy(f32[8,384,1536]{2,1,0:T(8,128)} %get-tuple-element.28) | data formatting | bytes 37748736
  628.8 4.6 copy-done.1
  633.4 6.8 %copy.15 = f32[8,1536,384]{2,1,0:T(8,128)} copy(f32[8,1536,384]{2,1,0:T(8,128)S(1)} %copy-done.1) | data formatting | bytes 37748736
Async XLA Ops:
  3.3 14.6 %copy-start = (f32[8,1536,384]{2,1,0:T(8,128)S(1)}, f32[8,1536,384]{2,1,0:T(8,128)}, u32[]{:S(2)}) copy-start(f32[8,1536,384]{2,1,0:T(8,128)} %w1.3) | copy-start | bytes 56623108
  3.4 28.6 %collective-permute-start.1 = (bf16[2,784,384]{2,1,0:T(8,128)(2,1)S(1)}, bf16[2,784,384]{2,1,0:T(8,128)(2,1)S(1)}, u32[]{:S(2)}, u32[]{:S(2)}) collective-permute-start(bf16[2,784,384]{2,1,0:T(8,128)(2,1)S(1)} %constant_dynamic-update-slice_fusion), channel_id=1, source_target_pairs={{0,8},{1,24},{2,10},{3,26},{4,12},{5,28},{6,14},{7,30},{8,0},{9,16... | collective-permute-start | bytes 3612680 | tf_op jit(solution)/shard_map/ppermute | solution.py:613
  6.5 112.6 %collective-permute-start = (bf16[2,784,384]{2,1,0:T(8,128)(2,1)S(1)}, bf16[2,784,384]{2,1,0:T(8,128)(2,1)S(1)}, u32[]{:S(2)}, u32[]{:S(2)}) collective-permute-start(bf16[2,784,384]{2,1,0:T(8,128)(2,1)S(1)} %constant_dynamic-update-slice_fusion), channel_id=1, source_target_pairs={{0,0},{1,16},{2,2},{3,18},{4,4},{5,20},{6,6},{7,22},{8,8},{9,24},{... | collective-permute-start | bytes 3612680 | tf_op jit(solution)/shard_map/ppermute | solution.py:612
  615.0 18.4 %copy-start.1 = (f32[8,1536,384]{2,1,0:T(8,128)S(1)}, f32[8,1536,384]{2,1,0:T(8,128)}, u32[]{:S(2)}) copy-start(f32[8,1536,384]{2,1,0:T(8,128)} %get-tuple-element.29) | copy-start | bytes 56623108

commit v4 on v3

--- a/solution.py
+++ b/solution.py
@@ -10,7 +10,7 @@
 L, T, D, F = 8, 784, 384, 1536
 FT = 256
 NT = F // FT
-RC, CC = 112, 128
+RC, CC = 16, 256
 SQRT_HALF = 0.5 ** 0.5
 INV_SQRT_2PI = 0.3989422804014327
 
@@ -47,9 +47,14 @@
         lay = step
         z_l = z_s.at[lay]
         h = h_s[lay]
-        for j in range(NT):
+        def pre(j):
             cols = slice(j * FT, (j + 1) * FT)
             z_l[:, cols] = dot(h, vin_ref[0, :, cols]).astype(BF16)
+
+        pre(0)
+        for j in range(NT):
+            if j + 1 < NT:
+                pre(j + 1)
             for rs, cs in chunks(j * FT):
                 a_s[rs, cs] = gelu_only(z_l[rs, cs].astype(F32)).astype(BF16)
         out = (h.astype(F32) + dot(a_s[...], vout_ref[0])).astype(BF16)
@@ -67,40 +72,77 @@
         z_l = z_s.at[lay]
         e = e_s[...]
         hT_s[...] = h_s[lay].T
-        for j in range(NT):
+        def up(j):
             cols = slice(j * FT, (j + 1) * FT)
             q_s[:, cols] = dot(e, vout_ref[0, cols, :], 1, 1).astype(BF16)
+
+        up(0)
+        for j in range(NT):
+            if j + 1 < NT:
+                up(j + 1)
             for rs, cs in chunks(j * FT):
                 act, slope = gelu_both(z_l[rs, cs].astype(F32))
                 a_s[rs, cs] = act.astype(BF16)
                 q_s[rs, cs] = (slope * q_s[rs, cs].astype(F32)).astype(BF16)
-            gout_ref[0, cols, :] = dot(a_s[:, cols], e, 0, 0).astype(BF16)
-            gin_ref[0, :, cols] = dot(hT_s[...], q_s[:, cols]).astype(BF16)
+        gout_ref[0] = dot(a_s[...], e, 0, 0).astype(BF16)
+        gin_ref[0] = dot(hT_s[...], q_s[...]).astype(BF16)
         e_s[...] = (e.astype(F32) + dot(q_s[...], vin_ref[0], 1, 1)).astype(BF16)
 
 
-def run_pass(x, y, vin, vout):
+def swap_pass_kernel(x_ref, y_ref, vin_ref, vout_ref, a0, a1, gin_ref, gout_ref, loss_ref, p0, p1, h_s, z_s, a_s, q_s, e_s, hT_s, s_sem, r_sem):
+    me = Place()
+    src, dst = (a0, a1), (p0, p1)
+
+    def copy(l, k):
+        return remote(half_at(src[k], k, l, 1 - me.core, 0, ROWS[k]), dst[k].at[l], s_sem.at[l, k], r_sem.at[l, k], me.partner)
+
+    @pl.when(pl.program_id(0) == 0)
+    def _():
+        me.barrier([me.partner])
+
+        def begin(l, _):
+            for k in (0, 1):
+                copy(l, k).start()
+            return 0
+        lax.fori_loop(0, L, begin, 0)
+    pass_kernel(x_ref, y_ref, vin_ref, vout_ref, gin_ref, gout_ref, loss_ref, h_s, z_s, a_s, q_s, e_s, hT_s)
+
+    @pl.when(pl.program_id(0) == 2 * L - 1)
+    def _():
+        def end(l, _):
+            for k in (0, 1):
+                copy(l, k).wait()
+            return 0
+        lax.fori_loop(0, L, end, 0)
+
+
+def run_pass(x, y, vin, vout, earlier=()):
     lay = lambda s: jnp.where(s < L, s, 2 * L - 1 - s)
     glay = lambda s: jnp.where(s < L, L - 1, 2 * L - 1 - s)
+    any_spec = pl.BlockSpec(memory_space=pl.ANY)
+    extra = [any_spec] * len(earlier)
+    landed = [jax.ShapeDtypeStruct((L, ROWS[k], COLS[k]), BF16) for k in range(len(earlier))]
+    sems = [pltpu.SemaphoreType.DMA((L, 2))] * len(earlier)
+    more = dict(collective_id=3, has_side_effects=True) if earlier else {}
     return pl.pallas_call(
-        pass_kernel,
+        swap_pass_kernel if earlier else pass_kernel,
         grid=(2 * L,),
         in_specs=[
             pl.BlockSpec((T, D), lambda s: (0, 0)),
             pl.BlockSpec((T, D), lambda s: (0, 0)),
             pl.BlockSpec((1, D, F), lambda s: (lay(s), 0, 0)),
             pl.BlockSpec((1, F, D), lambda s: (lay(s), 0, 0)),
-        ],
+        ] + extra,
         out_specs=[
             pl.BlockSpec((1, D, F), lambda s: (glay(s), 0, 0)),
             pl.BlockSpec((1, F, D), lambda s: (glay(s), 0, 0)),
             pl.BlockSpec(memory_space=pltpu.SMEM),
-        ],
+        ] + extra,
         out_shape=[
             jax.ShapeDtypeStruct((L, D, F), BF16),
             jax.ShapeDtypeStruct((L, F, D), BF16),
             jax.ShapeDtypeStruct((1, 1), F32),
-        ],
+        ] + landed,
         scratch_shapes=[
             pltpu.VMEM((L + 1, T, D), BF16),
             pltpu.VMEM((L, T, F), BF16),
@@ -108,10 +150,10 @@
             pltpu.VMEM((T, F), BF16),
             pltpu.VMEM((T, D), BF16),
             pltpu.VMEM((D, T), BF16),
-        ],
-        compiler_params=pltpu.CompilerParams(vmem_limit_bytes=60 * 2**20),
+        ] + sems,
+        compiler_params=pltpu.CompilerParams(vmem_limit_bytes=60 * 2**20, **more),
         cost_estimate=pl.CostEstimate(flops=L * 12 * T * D * F, bytes_accessed=4 * L * D * F * 2, transcendentals=0),
-    )(x, y, vin, vout)
+    )(x, y, vin, vout, *earlier)
 
 
 ROWS = (384, 768)
@@ -471,7 +513,7 @@
     )(x, y, vin, vout, w_in, w_out)
 
 
-def ascent_kernel(group, a0, a1, b0, b1, w0, w1, t0, t1, oa0, oa1, ob0, ob1, pa0, pa1, pb0, pb1, wb0, wb1, tb0, tb1, nt,
+def ascent_kernel(group, a0, a1, b0, b1, h0, h1, w0, w1, t0, t1, oa0, oa1, ob0, ob1, pa0, pa1, pb0, pb1, wb0, wb1, tb0, tb1, nt,
                   o_sem, p_sem, ps_sem, w_sem, tl_sem, ts_sem, tr_sem, n_sem):
     me = Place()
     core = me.core
@@ -484,6 +526,8 @@
         return pltpu.make_async_copy(half_at(src[i][k], k, l, core, 0, ROWS[k]), own[i][k].at[l], o_sem.at[l, k, i])
 
     def peer_copy(l, k, i):
+        if i == 0:
+            return pltpu.make_async_copy((h0, h1)[k].at[l], peer[0][k].at[l], p_sem.at[l, k, 0])
         return remote(half_at(src[i][k], k, l, 1 - core, 0, ROWS[k]), peer[i][k].at[l], ps_sem.at[l, k, i], p_sem.at[l, k, i], me.partner)
 
     def w_copy(l, k):
@@ -508,7 +552,7 @@
 
     def start_all(l, _):
         for k in kinds:
-            for i in range(2):
+            for i in (1, 0):
                 peer_copy(l, k, i).start()
                 own_copy(l, k, i).start()
         return 0
@@ -519,9 +563,10 @@
 
     def square_layer(l, acc):
         for k in kinds:
-            for i in range(2):
-                own_copy(l, k, i).wait()
-                peer_copy(l, k, i).wait_recv()
+            own_copy(l, k, 0).wait()
+            own_copy(l, k, 1).wait()
+            peer_copy(l, k, 0).wait()
+            peer_copy(l, k, 1).wait_recv()
 
             def body(i, tot, k=k):
                 g = mean_rows(l, k, al(i * 16, 16))
@@ -565,8 +610,7 @@
     def finish(l, _):
         for k in kinds:
             t_send(l, k).wait_recv()
-            for i in range(2):
-                peer_copy(l, k, i).wait_send()
+            peer_copy(l, k, 1).wait_send()
         return 0
     lax.fori_loop(0, L, finish, 0)
     for l in (L - 2, L - 1):
@@ -575,7 +619,7 @@
             t_send(l, k).wait_send()
 
 
-def ascent(group, first, second, w_in, w_out):
+def ascent(group, first, second, landed, w_in, w_out):
     def per_kind(lead, dtype):
         return [pltpu.VMEM((lead, ROWS[k], COLS[k]), dtype) for k in (0, 1)]
     dma = pltpu.SemaphoreType.DMA
@@ -584,12 +628,12 @@
                + [dma((L, 2, 2))] * 3 + [dma((2, 2))] * 3 + [dma((L, 2)), dma((2,))])
     return pl.pallas_call(
         functools.partial(ascent_kernel, group),
-        in_specs=[any_spec] * 6,
+        in_specs=[any_spec] * 8,
         out_specs=[any_spec] * 2,
         out_shape=[jax.ShapeDtypeStruct((L, D, F), BF16), jax.ShapeDtypeStruct((L, F, D), BF16)],
         scratch_shapes=scratch,
         compiler_params=pltpu.CompilerParams(collective_id=2, has_side_effects=True, vmem_limit_bytes=60 * 2**20),
-    )(*first, *second, w_in, w_out)
+    )(*first, *second, *landed, w_in, w_out)
 
 
 def move_pairs(sub_size, data_size, flip):
@@ -597,8 +641,8 @@
     for shard in range(sub_size):
         for data_idx in range(data_size):
             group = data_idx % 2
-            chip = 2 * group + ((shard + flip) % 2)
-            pairs.append((shard * data_size + data_idx, chip * data_size + data_idx - group + shard // 2))
+            chip = 2 * ((shard // 2 + flip) % 2) + group
+            pairs.append((shard * data_size + data_idx, chip * data_size + data_idx - group + shard % 2))
     return pairs
 
 
@@ -612,9 +656,9 @@
         own = lax.ppermute(tok, axes, move_pairs(sub_size, data_size, 0))
         other = lax.ppermute(tok, axes, move_pairs(sub_size, data_size, 1))
         v_in, v_out = w_in.astype(BF16), w_out.astype(BF16)
-        first = run_pass(own[0], own[1], v_in, v_out)[:2]
-        second = run_pass(other[0], other[1], v_in, v_out)[:2]
-        t_in, t_out = ascent(sub_size, first, second, w_in, w_out)
+        first = tuple(run_pass(own[0], own[1], v_in, v_out)[:2])
+        second = run_pass(other[0], other[1], v_in, v_out, first)
+        t_in, t_out = ascent(sub_size, first, second[:2], second[3:], w_in, w_out)
         new_in, new_out, loss_all = last_pass(dev_count, own[0], own[1], t_in, t_out, w_in, w_out)
         return new_in, new_out, loss_all[0, 0]
 

time: 640 us -> 600 us (0.938)
  Pallas kernels: 580 us -> 549 us
  waiting for transfers between devices: 9.59 us -> 0.01 us
    pallas_call x1, Pallas kernels: 48.9 us -> 32.6 us  [ascent(): pl.pallas_call(functools.partial(ascent_kernel, group), in_specs=[any_spe...]
    pallas_call x2, Pallas kernels: 172 us -> 160 us  [run_pass(): pl.pallas_call(swap_pass_kernel if earlier else pass_kernel, grid=(2 * L,...]
    ppermute x1, waiting for transfers between devices: 9.59 us -> 0.01 us  [device_step(): other = lax.ppermute(tok, axes, move_pairs(sub_size, data_size, 1))]
  transfers between devices with their start and end apart: 2 -> 2, of which waited for: 1 -> 0; matrix products, arithmetic and copies ran while one was open for 3% -> 3% of each run, Pallas kernels for 13% -> 12%
where the time goes in v4:
time: 600 us
  Pallas kernels  549 us (92%)
  local copies, waits for them, and re-layouts  31.4 us (5%)
  other arithmetic  14.5 us (2%)
    pallas_call x1, Pallas kernels, last_pass(): pl.pallas_call(functools.partial(last_kernel, count), grid=(2 * L,), in_s...  356 us
    pallas_call x2, Pallas kernels, run_pass(): pl.pallas_call(swap_pass_kernel if earlier else pass_kernel, grid=(2 * L,...  160 us
    pallas_call x1, Pallas kernels, ascent(): pl.pallas_call(functools.partial(ascent_kernel, group), in_specs=[any_spe...  32.6 us
    unnamed x9, local copies, waits for them, and re-layouts  27.6 us
    convert_element_type x2, other arithmetic, device_step(): v_in, v_out = (w_in.astype(BF16), w_out.astype(BF16))  14.5 us
  transfers between devices with their start and end apart: 2, of which 0 were waited for; matrix products, arithmetic and copies ran while one was open for 3% of the time, Pallas kernels for 12%

profile of v4, /device:TPU:0, one launch (start us, length us, event | category | flops | bytes accessed | tf_op | source)
XLA Modules:
  0.0 600.2 jit_solution(9563610849596553336)
XLA Ops:
  0.6 1.1 copy.9
  1.8 0.1 stack_reshape.6
  1.9 0.1 constant_dynamic-update-slice_fusion.1
  2.0 1.1 copy.10
  3.1 0.1 stack_reshape.7
  3.2 0.1 constant_dynamic-update-slice_fusion
  3.3 0.0 copy-start
  3.4 0.9 collective-permute-start
  4.2 4.2 collective-permute-start.1
  8.4 10.1 %convert_element_type.6.vin_ref = bf16[8,384,1536]{2,1,0:T(8,128)(2,1)} convert(f32[8,384,1536]{2,1,0:T(8,128)} %w0.3) | non-fusion elementwise | flops 4718592 | bytes 28311552 | tf_op jit(solution)/shard_map/convert_element_type | solution.py:658
  18.5 0.0 copy-done
  18.6 4.4 convert_element_type.7.vout_ref
  22.9 0.0 collective-permute-done
  22.9 1.1 slice_bitcast_fusion.2
  24.1 73.7 %shard_map.67 = (bf16[8,384,1536]{2,1,0:T(8,128)(2,1)}, bf16[8,1536,384]{2,1,0:T(8,128)(2,1)}, f32[1,1]{1,0:T(1,128)}) custom-call(bf16[784,384]{1,0:T(8,128)(2,1)} %get-tuple-element.28.x_ref, bf16[784,384]{1,0:T(8,128)(2,1)} %get-tuple-element.27.y_ref, bf16[8,384,1536]{2,1,0:T(8,128)(2,1)} %convert_element_type.6.vin_ref, ...), custom_call_target="tpu_custom_call" | custom-call | flops 44392513536 | bytes 37748736 | tf_op jit(solution)/shard_map/pallas_call | solution.py:127
  97.7 0.0 collective-permute-done.1
  97.8 1.2 slice_bitcast_fusion
  98.9 86.2 %shard_map.68 = (bf16[8,384,1536]{2,1,0:T(8,128)(2,1)}, bf16[8,1536,384]{2,1,0:T(8,128)(2,1)}, f32[1,1]{1,0:T(1,128)}, bf16[8,384,768]{2,1,0:T(8,128)(2,1)}, bf16[8,768,384]{2,1,0:T(8,128)(2,1)}) custom-call(bf16[784,384]{1,0:T(8,128)(2,1)} %get-tuple-element.26.x_ref, bf16[784,384]{1,0:T(8,128)(2,1)} %get-tuple-element.25.y_ref, ...), custom_call_target="tpu_custom_call" | custom-call | flops 44392513536 | bytes 37748736 | tf_op jit(solution)/shard_map/pallas_call | solution.py:127
  185.2 32.6 %shard_map.69 = (bf16[8,384,1536]{2,1,0:T(8,128)(2,1)}, bf16[8,1536,384]{2,1,0:T(8,128)(2,1)}) custom-call(bf16[8,384,1536]{2,1,0:T(8,128)(2,1)} %get-tuple-element.14.a0, bf16[8,1536,384]{2,1,0:T(8,128)(2,1)} %get-tuple-element.15.a1, bf16[8,384,1536]{2,1,0:T(8,128)(2,1)} %get-tuple-element.16.b0, bf16[8,1536,384]{2,1,0:T(8,128)(2,1)} %get-tuple-element.17.b1, ...), custom_call_target="tpu_custom_call" | custom-call | tf_op jit(solution)/shard_map/pallas_call | solution.py:629
  217.8 356.0 %shard_map.70 = (f32[8,384,1536]{2,1,0:T(8,128)}, f32[8,1536,384]{2,1,0:T(8,128)}, f32[8,128]{1,0:T(8,128)}) custom-call(bf16[784,384]{1,0:T(8,128)(2,1)} %get-tuple-element.28.x_ref, bf16[784,384]{1,0:T(8,128)(2,1)} %get-tuple-element.27.y_ref, bf16[8,384,1536]{2,1,0:T(8,128)(2,1)} %get-tuple-element.20.vin_ref, ...), custom_call_target="tpu_custom_call" | custom-call | tf_op jit(solution)/shard_map/pallas_call | solution.py:498
  573.8 1.2 slice.21
  575.0 0.0 copy-start.1
  575.0 13.7 %copy.14 = f32[8,384,1536]{2,1,0:T(8,128)} copy(f32[8,384,1536]{2,1,0:T(8,128)} %get-tuple-element.32) | data formatting | bytes 37748736
  588.8 4.6 copy-done.1
  593.4 6.8 %copy.15 = f32[8,1536,384]{2,1,0:T(8,128)} copy(f32[8,1536,384]{2,1,0:T(8,128)S(1)} %copy-done.1) | data formatting | bytes 37748736
Async XLA Ops:
  3.3 15.2 %copy-start = (f32[8,1536,384]{2,1,0:T(8,128)S(1)}, f32[8,1536,384]{2,1,0:T(8,128)}, u32[]{:S(2)}) copy-start(f32[8,1536,384]{2,1,0:T(8,128)} %w1.3) | copy-start | bytes 56623108
  3.4 19.6 %collective-permute-start = (bf16[2,784,384]{2,1,0:T(8,128)(2,1)S(1)}, bf16[2,784,384]{2,1,0:T(8,128)(2,1)S(1)}, u32[]{:S(2)}, u32[]{:S(2)}) collective-permute-start(bf16[2,784,384]{2,1,0:T(8,128)(2,1)S(1)} %constant_dynamic-update-slice_fusion), channel_id=1, source_target_pairs={{0,0},{1,8},{2,2},{3,10},{4,4},{5,12},{6,6},{7,14},{8,1},{9,9},{10... | collective-permute-start | bytes 3612680 | tf_op jit(solution)/shard_map/ppermute | solution.py:656
  4.2 93.5 %collective-permute-start.1 = (bf16[2,784,384]{2,1,0:T(8,128)(2,1)S(1)}, bf16[2,784,384]{2,1,0:T(8,128)(2,1)S(1)}, u32[]{:S(2)}, u32[]{:S(2)}) collective-permute-start(bf16[2,784,384]{2,1,0:T(8,128)(2,1)S(1)} %constant_dynamic-update-slice_fusion), channel_id=1, source_target_pairs={{0,16},{1,24},{2,18},{3,26},{4,20},{5,28},{6,22},{7,30},{8,17},{9,... | collective-permute-start | bytes 3612680 | tf_op jit(solution)/shard_map/ppermute | solution.py:657
  575.0 18.4 %copy-start.1 = (f32[8,1536,384]{2,1,0:T(8,128)S(1)}, f32[8,1536,384]{2,1,0:T(8,128)}, u32[]{:S(2)}) copy-start(f32[8,1536,384]{2,1,0:T(8,128)} %get-tuple-element.33) | copy-start | bytes 56623108

commit v5 on v4

--- a/solution.py
+++ b/solution.py
@@ -96,18 +96,19 @@
     def copy(l, k):
         return remote(half_at(src[k], k, l, 1 - me.core, 0, ROWS[k]), dst[k].at[l], s_sem.at[l, k], r_sem.at[l, k], me.partner)
 
-    @pl.when(pl.program_id(0) == 0)
+    step = pl.program_id(0)
+
+    @pl.when(step == 0)
     def _():
         me.barrier([me.partner])
 
-        def begin(l, _):
-            for k in (0, 1):
-                copy(l, k).start()
-            return 0
-        lax.fori_loop(0, L, begin, 0)
+    @pl.when(step < L)
+    def _():
+        for k in (0, 1):
+            copy(step, k).start()
     pass_kernel(x_ref, y_ref, vin_ref, vout_ref, gin_ref, gout_ref, loss_ref, h_s, z_s, a_s, q_s, e_s, hT_s)
 
-    @pl.when(pl.program_id(0) == 2 * L - 1)
+    @pl.when(step == 2 * L - 1)
     def _():
         def end(l, _):
             for k in (0, 1):

time: 600 us -> 601 us (level)
  no operation moved by 1% of the time
where the time goes in v5:
time: 601 us; the launch traced here: 600 us
  Pallas kernels  549 us (91%)
  local copies, waits for them, and re-layouts  31.4 us (5%)
  other arithmetic  14.5 us (2%)
    pallas_call x1, Pallas kernels, last_pass(): pl.pallas_call(functools.partial(last_kernel, count), grid=(2 * L,), in_s...  356 us
    pallas_call x2, Pallas kernels, run_pass(): pl.pallas_call(swap_pass_kernel if earlier else pass_kernel, grid=(2 * L,...  160 us
    pallas_call x1, Pallas kernels, ascent(): pl.pallas_call(functools.partial(ascent_kernel, group), in_specs=[any_spe...  32.6 us
    unnamed x9, local copies, waits for them, and re-layouts  27.6 us
    convert_element_type x2, other arithmetic, device_step(): v_in, v_out = (w_in.astype(BF16), w_out.astype(BF16))  14.5 us
  transfers between devices with their start and end apart: 2, of which 0 were waited for; matrix products, arithmetic and copies ran while one was open for 3% of the time, Pallas kernels for 12%

profile of v5, /device:TPU:0, one launch (start us, length us, event | category | flops | bytes accessed | tf_op | source)
XLA Modules:
  0.0 600.4 jit_solution(5353992265525676410)
XLA Ops:
  0.6 1.1 copy.9
  1.8 0.1 stack_reshape.6
  1.9 0.1 constant_dynamic-update-slice_fusion.1
  2.0 1.1 copy.10
  3.1 0.1 stack_reshape.7
  3.2 0.1 constant_dynamic-update-slice_fusion
  3.3 0.0 copy-start
  3.4 0.9 collective-permute-start
  4.2 4.2 collective-permute-start.1
  8.4 10.1 %convert_element_type.6.vin_ref = bf16[8,384,1536]{2,1,0:T(8,128)(2,1)} convert(f32[8,384,1536]{2,1,0:T(8,128)} %w0.3) | non-fusion elementwise | flops 4718592 | bytes 28311552 | tf_op jit(solution)/shard_map/convert_element_type | solution.py:659
  18.5 0.0 copy-done
  18.6 4.4 convert_element_type.7.vout_ref
  22.9 0.0 collective-permute-done
  22.9 1.1 slice_bitcast_fusion.2
  24.1 73.7 %shard_map.67 = (bf16[8,384,1536]{2,1,0:T(8,128)(2,1)}, bf16[8,1536,384]{2,1,0:T(8,128)(2,1)}, f32[1,1]{1,0:T(1,128)}) custom-call(bf16[784,384]{1,0:T(8,128)(2,1)} %get-tuple-element.28.x_ref, bf16[784,384]{1,0:T(8,128)(2,1)} %get-tuple-element.27.y_ref, bf16[8,384,1536]{2,1,0:T(8,128)(2,1)} %convert_element_type.6.vin_ref, ...), custom_call_target="tpu_custom_call" | custom-call | flops 44392513536 | bytes 37748736 | tf_op jit(solution)/shard_map/pallas_call | solution.py:128
  97.7 0.0 collective-permute-done.1
  97.8 1.2 slice_bitcast_fusion
  98.9 86.5 %shard_map.68 = (bf16[8,384,1536]{2,1,0:T(8,128)(2,1)}, bf16[8,1536,384]{2,1,0:T(8,128)(2,1)}, f32[1,1]{1,0:T(1,128)}, bf16[8,384,768]{2,1,0:T(8,128)(2,1)}, bf16[8,768,384]{2,1,0:T(8,128)(2,1)}) custom-call(bf16[784,384]{1,0:T(8,128)(2,1)} %get-tuple-element.26.x_ref, bf16[784,384]{1,0:T(8,128)(2,1)} %get-tuple-element.25.y_ref, ...), custom_call_target="tpu_custom_call" | custom-call | flops 44392513536 | bytes 37748736 | tf_op jit(solution)/shard_map/pallas_call | solution.py:128
  185.4 32.6 %shard_map.69 = (bf16[8,384,1536]{2,1,0:T(8,128)(2,1)}, bf16[8,1536,384]{2,1,0:T(8,128)(2,1)}) custom-call(bf16[8,384,1536]{2,1,0:T(8,128)(2,1)} %get-tuple-element.14.a0, bf16[8,1536,384]{2,1,0:T(8,128)(2,1)} %get-tuple-element.15.a1, bf16[8,384,1536]{2,1,0:T(8,128)(2,1)} %get-tuple-element.16.b0, bf16[8,1536,384]{2,1,0:T(8,128)(2,1)} %get-tuple-element.17.b1, ...), custom_call_target="tpu_custom_call" | custom-call | tf_op jit(solution)/shard_map/pallas_call | solution.py:630
  218.0 356.0 %shard_map.70 = (f32[8,384,1536]{2,1,0:T(8,128)}, f32[8,1536,384]{2,1,0:T(8,128)}, f32[8,128]{1,0:T(8,128)}) custom-call(bf16[784,384]{1,0:T(8,128)(2,1)} %get-tuple-element.28.x_ref, bf16[784,384]{1,0:T(8,128)(2,1)} %get-tuple-element.27.y_ref, bf16[8,384,1536]{2,1,0:T(8,128)(2,1)} %get-tuple-element.20.vin_ref, ...), custom_call_target="tpu_custom_call" | custom-call | tf_op jit(solution)/shard_map/pallas_call | solution.py:499
  574.0 1.2 slice.21
  575.2 0.0 copy-start.1
  575.2 13.7 %copy.14 = f32[8,384,1536]{2,1,0:T(8,128)} copy(f32[8,384,1536]{2,1,0:T(8,128)} %get-tuple-element.32) | data formatting | bytes 37748736
  589.0 4.6 copy-done.1
  593.6 6.8 %copy.15 = f32[8,1536,384]{2,1,0:T(8,128)} copy(f32[8,1536,384]{2,1,0:T(8,128)S(1)} %copy-done.1) | data formatting | bytes 37748736
Async XLA Ops:
  3.3 15.2 %copy-start = (f32[8,1536,384]{2,1,0:T(8,128)S(1)}, f32[8,1536,384]{2,1,0:T(8,128)}, u32[]{:S(2)}) copy-start(f32[8,1536,384]{2,1,0:T(8,128)} %w1.3) | copy-start | bytes 56623108
  3.4 19.6 %collective-permute-start = (bf16[2,784,384]{2,1,0:T(8,128)(2,1)S(1)}, bf16[2,784,384]{2,1,0:T(8,128)(2,1)S(1)}, u32[]{:S(2)}, u32[]{:S(2)}) collective-permute-start(bf16[2,784,384]{2,1,0:T(8,128)(2,1)S(1)} %constant_dynamic-update-slice_fusion), channel_id=1, source_target_pairs={{0,0},{1,8},{2,2},{3,10},{4,4},{5,12},{6,6},{7,14},{8,1},{9,9},{10... | collective-permute-start | bytes 3612680 | tf_op jit(solution)/shard_map/ppermute | solution.py:657
  4.2 93.5 %collective-permute-start.1 = (bf16[2,784,384]{2,1,0:T(8,128)(2,1)S(1)}, bf16[2,784,384]{2,1,0:T(8,128)(2,1)S(1)}, u32[]{:S(2)}, u32[]{:S(2)}) collective-permute-start(bf16[2,784,384]{2,1,0:T(8,128)(2,1)S(1)} %constant_dynamic-update-slice_fusion), channel_id=1, source_target_pairs={{0,16},{1,24},{2,18},{3,26},{4,20},{5,28},{6,22},{7,30},{8,17},{9,... | collective-permute-start | bytes 3612680 | tf_op jit(solution)/shard_map/ppermute | solution.py:658
  575.2 18.4 %copy-start.1 = (f32[8,1536,384]{2,1,0:T(8,128)S(1)}, f32[8,1536,384]{2,1,0:T(8,128)}, u32[]{:S(2)}) copy-start(f32[8,1536,384]{2,1,0:T(8,128)} %get-tuple-element.33) | copy-start | bytes 56623108
